TPU v7x, 32 devices: a whole 2x2x4 slice. The times are simulated.
32 devices in a mesh: batch: 4 (over z), grid: 8 (over y, x, core).
Axes of the slice: x: 2, y: 2, z: 4, core: 2. Of those that a mesh axis runs over, the one named last changes fastest.
Arguments:
- fields: bfloat16 [1024, 512, 512], P(('batch', 'grid')), parts along dimension 0, may hold values from -18 to 18
- norm_gain: float32 [256], replicated, may hold values from 0.5 to 1.5
- norm_shift: float32 [256], replicated, may hold values from -3 to 3
- first_weight: bfloat16 [2, 8, 32, 32], replicated, may hold values from -0.75 to 0.75
- second_weight: bfloat16 [2, 8, 32, 32], replicated, may hold values from -0.75 to 0.75
- first_bias: float32 [2, 256], replicated, may hold values from -2 to 2
Outputs:
- mixed_fields: bfloat16 [1024, 512, 512], P(('batch', 'grid')), parts along dimension 0
There are 4 independent parts, one for each index of `batch`. A program takes and returns all parts, laid end to end along the dimension named above; an argument that names none is the same for every part. Nothing has to cross between parts.
All inputs are finite; a program needn't handle non-finite values.
Results may differ from a plain program's by a relative error of at most 0.0055.
Values may be sent and summed in bfloat16 or wider, within the bound.
A program may use at most 192 MiB of HBM per device.

v0:
```python
import functools
import math

import jax
import jax.numpy as jnp
import numpy as np
from jax import lax
from jax.experimental import pallas as pl
from jax.experimental.pallas import tpu as pltpu
from jax.sharding import PartitionSpec as P


def tables(rows, cols):
    half = cols // 2
    col_index = jnp.arange(cols, dtype=jnp.int32)
    mode_index = jnp.arange(half, dtype=jnp.int32)
    angle_w = (col_index[:, None] * mode_index[None, :] % cols).astype(jnp.float32) * (
        2.0 * math.pi / cols
    )
    scale_w = 1.0 / math.sqrt(cols)
    fwd_w = jnp.concatenate(
        [jnp.cos(angle_w) * scale_w, -jnp.sin(angle_w) * scale_w], axis=1
    ).astype(jnp.bfloat16)
    weight_k = jnp.where(mode_index == 0, 1.0, 2.0).astype(jnp.float32)
    inv_w = jnp.concatenate(
        [
            (jnp.cos(angle_w) * weight_k[None, :] * scale_w).T,
            (-jnp.sin(angle_w) * weight_k[None, :] * scale_w).T,
        ],
        axis=0,
    ).astype(jnp.bfloat16)
    row_index = jnp.arange(rows, dtype=jnp.int32)
    angle_h = (row_index[:, None] * row_index[None, :] % rows).astype(jnp.float32) * (
        2.0 * math.pi / rows
    )
    scale_h = 1.0 / math.sqrt(rows)
    cos_h = (jnp.cos(angle_h) * scale_h).astype(jnp.bfloat16)
    sin_h = (jnp.sin(angle_h) * scale_h).astype(jnp.bfloat16)
    return (fwd_w, inv_w, cos_h, sin_h)


def mult(form, left, right):
    return jnp.einsum(form, left, right, preferred_element_type=jnp.float32)


def shrink(values):
    return jnp.maximum(values - 0.01, 0.0) + jnp.minimum(values + 0.01, 0.0)


def mix_modes(real_part, imag_part, first_weight, second_weight, first_bias):
    blocks = first_weight.shape[1]
    width = first_weight.shape[2]
    shape = real_part.shape
    real_blk = real_part.reshape(blocks, width, -1)
    imag_blk = imag_part.reshape(blocks, width, -1)
    bias_blk = first_bias.reshape(2, blocks, width, 1)
    hid_re = jax.nn.relu(
        mult("bio,bim->bom", first_weight[0], real_blk)
        - mult("bio,bim->bom", first_weight[1], imag_blk)
        + bias_blk[0]
    ).astype(jnp.bfloat16)
    hid_im = jax.nn.relu(
        mult("bio,bim->bom", first_weight[0], imag_blk)
        + mult("bio,bim->bom", first_weight[1], real_blk)
        + bias_blk[1]
    ).astype(jnp.bfloat16)
    out_re = mult("bio,bim->bom", second_weight[0], hid_re) - mult(
        "bio,bim->bom", second_weight[1], hid_im
    )
    out_im = mult("bio,bim->bom", second_weight[0], hid_im) + mult(
        "bio,bim->bom", second_weight[1], hid_re
    )
    return (
        shrink(out_re).astype(jnp.bfloat16).reshape(shape),
        shrink(out_im).astype(jnp.bfloat16).reshape(shape),
    )


def per_device(fields, norm_gain, norm_shift, first_weight, second_weight, first_bias):
    local_ch, rows, cols = fields.shape
    half = cols // 2
    groups = lax.axis_size("grid")
    channels = local_ch * groups
    fwd_w, inv_w, cos_h, sin_h = tables(rows, cols)
    values = fields.astype(jnp.float32)
    start = lax.axis_index("grid") * local_ch
    gain_own = lax.dynamic_slice_in_dim(norm_gain, start, local_ch)
    shift_own = lax.dynamic_slice_in_dim(norm_shift, start, local_ch)
    total_sum, total_sq = lax.psum(
        (jnp.sum(values, axis=0), jnp.sum(values * values, axis=0)), "grid"
    )
    mean = total_sum / channels
    var = total_sq / channels - mean * mean
    normed = (
        (values - mean) * lax.rsqrt(var + 1e-05) * gain_own[:, None, None]
        + shift_own[:, None, None]
    ).astype(jnp.bfloat16)
    along_w = (
        mult("chw,wk->chk", normed, fwd_w).astype(jnp.bfloat16).reshape(local_ch, rows, 2, half)
    )
    first_p = mult("kh,chpq->ckpq", cos_h, along_w)
    first_q = mult("kh,chpq->ckpq", sin_h, along_w)
    modes = jnp.stack(
        [
            (first_p[:, :, 0] + first_q[:, :, 1]).astype(jnp.bfloat16),
            (first_p[:, :, 1] - first_q[:, :, 0]).astype(jnp.bfloat16),
        ],
        axis=2,
    )
    spread = lax.all_to_all(modes, "grid", split_axis=1, concat_axis=0, tiled=True)
    shr_re, shr_im = mix_modes(
        spread[:, :, 0], spread[:, :, 1], first_weight, second_weight, first_bias
    )
    gathered = lax.all_to_all(
        jnp.stack([shr_re, shr_im], axis=2), "grid", split_axis=0, concat_axis=1, tiled=True
    )
    back_p = mult("kh,ckpq->chpq", cos_h, gathered)
    back_q = mult("kh,ckpq->chpq", sin_h, gathered)
    back_re = (back_p[:, :, 0] - back_q[:, :, 1]).astype(jnp.bfloat16)
    back_im = (back_p[:, :, 1] + back_q[:, :, 0]).astype(jnp.bfloat16)
    backed = jnp.concatenate([back_re, back_im], axis=2)
    filtered = mult("chk,kw->chw", backed, inv_w)
    return (values + filtered).astype(jnp.bfloat16)

SUB = 8


def constant_tables(rows, cols):
    half, mid = cols // 2, rows // 2
    wave = lambda f, left, right, period: f(
        (left[:, None] * right[None, :] % period).astype(np.float32)
        * np.float32(2.0 * math.pi / period)
    ) * np.float32(1.0 / math.sqrt(period))
    col, mode = np.arange(cols), np.arange(half)
    fwd_w = np.concatenate(
        [wave(np.cos, col, mode, cols), -wave(np.sin, col, mode, cols)], axis=1
    )
    weight_k = np.where(mode == 0, 1.0, 2.0).astype(np.float32)[:, None]
    inv_w = np.concatenate(
        [
            wave(np.cos, mode, col, cols) * weight_k,
            -wave(np.sin, mode, col, cols) * weight_k,
        ],
        axis=0,
    )
    row = np.arange(rows)
    cos_h, sin_h = wave(np.cos, row, row, rows), wave(np.sin, row, row, rows)
    low = np.concatenate([cos_h[: mid + 1], sin_h[1:mid]], axis=0)
    order = np.concatenate([row[: mid + 1], row[mid + 1 :][::-1]])
    swap = np.zeros((mid, mid), np.float32)
    swap[row[:mid], (mid - row[:mid]) % mid] = 1.0
    return tuple(t.astype(jnp.bfloat16) for t in (fwd_w, inv_w, low, low[:, order], swap))


def spread_weight(weight):
    size = weight.shape[0]
    rows = lax.broadcasted_iota(jnp.int32, (size * SUB, size), 0)
    cols = lax.broadcasted_iota(jnp.int32, (size * SUB, size), 1)
    repeat = jnp.where((rows >= cols * SUB) & (rows < cols * SUB + SUB), 1.0, 0.0).astype(
        jnp.bfloat16
    )
    last = (((1,), (1,)), ((), ()))
    tall = lax.dot_general(repeat, weight, last, preferred_element_type=jnp.float32)
    full = lax.dot_general(
        tall.astype(jnp.bfloat16), repeat, last, preferred_element_type=jnp.float32
    )
    left = lax.broadcasted_iota(jnp.int32, full.shape, 0)
    right = lax.broadcasted_iota(jnp.int32, full.shape, 1)
    return jnp.where(((left ^ right) & (SUB - 1)) == 0, full, 0.0).astype(jnp.bfloat16)


def stats_kernel(n, channels, sum_ref, sq_ref, out_ref, near, part, far, s1, r1, s2, r2, s3, r3, s4, r4):
    me = lax.axis_index("grid")
    chips = n // 2
    core, chip = lax.rem(me, 2), lax.div(me, 2)
    other = 1 - core
    sibling = chip * 2 + other
    rows = sum_ref.shape[0]
    half, piece = rows // 2, rows // n

    def ahead(j):
        return lax.rem(chip + j, chips)

    def span(c, k):
        return pl.ds(pl.multiple_of(c * half + k * piece, 8), piece)

    def send(source, target, send_sem, recv_sem, device):
        copy = pltpu.make_async_remote_copy(
            src_ref=source,
            dst_ref=target,
            send_sem=send_sem,
            recv_sem=recv_sem,
            device_id={"grid": device},
            device_id_type=pl.DeviceIdType.MESH,
        )
        copy.start()
        return copy

    barrier = pltpu.get_barrier_semaphore()
    for device in [sibling] + [ahead(j) * 2 + core for j in range(1, chips)]:
        pl.semaphore_signal(
            barrier, inc=1, device_id={"grid": device}, device_id_type=pl.DeviceIdType.MESH
        )
    pl.semaphore_wait(barrier, chips)

    theirs = pl.ds(pl.multiple_of(other * half, 8), half)
    first = [
        send(ref.at[theirs], near.at[i], s1.at[i], r1.at[i], sibling)
        for i, ref in enumerate((sum_ref, sq_ref))
    ]
    for copy in first:
        copy.wait_recv()
    second = []
    for j in range(1, chips + 1):
        k = ahead(j)
        local = pl.ds(pl.multiple_of(k * piece, 8), piece)
        for i, ref in enumerate((sum_ref, sq_ref)):
            part[j - 1, i] = ref[span(core, k)] + near[i, local]
    for j in range(1, chips):
        second.append(
            send(part.at[j - 1], far.at[j - 1], s2.at[j - 1], r2.at[j - 1], ahead(j) * 2 + core)
        )
    total_sum, total_sq = part[chips - 1, 0], part[chips - 1, 1]
    for j in range(1, chips):
        second[j - 1].wait_recv()
        total_sum = total_sum + far[j - 1, 0]
        total_sq = total_sq + far[j - 1, 1]
    mean = total_sum * (1.0 / channels)
    mine = span(core, chip)
    out_ref[0, mine] = mean
    out_ref[1, mine] = lax.rsqrt(total_sq * (1.0 / channels) - mean * mean + 1e-05)
    block = out_ref.at[:, mine]
    third = [
        send(block, block, s3.at[j - 1], r3.at[j - 1], ahead(j) * 2 + core)
        for j in range(1, chips)
    ]
    fourth = [send(block, block, s4.at[0], r4.at[0], sibling)]
    for j in range(1, chips):
        third[j - 1].wait_recv()
        block = out_ref.at[:, span(core, ahead(chips - j))]
        fourth.append(send(block, block, s4.at[j], r4.at[j], sibling))
    for copy in fourth:
        copy.wait_recv()
    for copy in first + second + third + fourth:
        copy.wait_send()


def shared_stats(total_sum, total_sq, n, channels):
    rows, cols = total_sum.shape
    chips = n // 2
    vmem = pl.BlockSpec(memory_space=pltpu.VMEM)
    counts = (2, chips - 1, chips - 1, chips)
    return pl.pallas_call(
        functools.partial(stats_kernel, n, channels),
        out_shape=jax.ShapeDtypeStruct((2, rows, cols), jnp.float32),
        in_specs=[vmem, vmem],
        out_specs=vmem,
        scratch_shapes=[
            pltpu.VMEM((2, rows // 2, cols), jnp.float32),
            pltpu.VMEM((chips, 2, rows // n, cols), jnp.float32),
            pltpu.VMEM((chips - 1, 2, rows // n, cols), jnp.float32),
        ]
        + [pltpu.SemaphoreType.DMA((c,)) for c in counts for _ in range(2)],
        compiler_params=pltpu.CompilerParams(
            collective_id=0, has_side_effects=True, vmem_limit_bytes=32 * 1024 * 1024
        ),
        name="stats",
    )(total_sum, total_sq)


def split_rows(total, sign):
    mid, half = total.shape[0] // 2, total.shape[1] // 2
    p_re, p_im = total[:mid, :half], total[:mid, half:]
    q_re, q_im = total[mid:, :half], total[mid:, half:]
    edge = lax.broadcasted_iota(jnp.int32, (mid, half), 0) == 0
    t_re = jnp.where(edge, 0.0, q_re)
    t_im = jnp.where(edge, 0.0, q_im)
    if sign < 0:
        t_re, t_im = -t_re, -t_im
    plus = (p_re + t_im, p_im - t_re)
    minus = (
        jnp.where(edge, q_re, p_re - t_im),
        jnp.where(edge, q_im, p_im + t_re),
    )
    return plus, minus


def forward_kernel(x_ref, stats_ref, gain_ref, shift_ref, fw_ref, fh_ref, out_ref):
    count, rows, cols = x_ref.shape
    mid, half = rows // 2, cols // 2
    start = (lax.axis_index("grid") * pl.num_programs(0) + pl.program_id(0)) * count
    for n in range(count):
        gain = gain_ref[start + n]
        shift = shift_ref[start + n]
        values = x_ref[n].astype(jnp.float32)
        normed = ((values - stats_ref[0]) * stats_ref[1] * gain + shift).astype(jnp.bfloat16)
        along = jnp.dot(normed, fw_ref[...], preferred_element_type=jnp.float32).astype(
            jnp.bfloat16
        )
        total = jnp.dot(fh_ref[...], along, preferred_element_type=jnp.float32)
        plus, minus = split_rows(total, 1)
        for place, pair in ((0, plus), (mid, minus)):
            for side in range(2):
                out_ref[n, place : place + mid, side * half : (side + 1) * half] = pair[
                    side
                ].astype(jnp.bfloat16)


def mix_kernel(x_ref, first_ref, second_ref, bias_ref, out_ref, w1_ref, w2_ref, b1_ref):
    @pl.when(pl.program_id(1) == 0)
    def _():
        block = lax.axis_index("grid") * pl.num_programs(0) + pl.program_id(0)
        width = first_ref.shape[2]
        size = width * SUB
        for source, target in ((first_ref, w1_ref), (second_ref, w2_ref)):
            real = spread_weight(source[0, block])
            imag = spread_weight(source[1, block])
            target[:size, :size] = real
            target[:size, size:] = -imag
            target[size:, :size] = imag
            target[size:, size:] = real
        shape = (size, bias_ref.shape[1])
        first = (lax.broadcasted_iota(jnp.int32, shape, 1) - block * width) * SUB
        offset = lax.broadcasted_iota(jnp.int32, shape, 0) - first
        own = (offset >= 0) & (offset < SUB)
        for side in range(2):
            picked = jnp.where(own, bias_ref[side : side + 1, :], 0.0)
            b1_ref[side * size : (side + 1) * size, :] = jnp.sum(picked, axis=1, keepdims=True)

    width, depth, cols = x_ref.shape
    half = cols // 2
    size = width * SUB
    for g in range(depth // (2 * SUB)):
        base = g * 2 * SUB
        values = x_ref[:, base : base + 2 * SUB, :].astype(jnp.float32)
        parts = []
        for s in range(2):
            flat = values[:, s * SUB : (s + 1) * SUB, :].reshape(size, cols).astype(jnp.bfloat16)
            both = jnp.concatenate([flat[:, :half], flat[:, half:]], axis=0)
            hid = jnp.dot(w1_ref[...], both, preferred_element_type=jnp.float32)
            hid = jnp.maximum(hid + b1_ref[...], 0.0).astype(jnp.bfloat16)
            mixed = jnp.dot(w2_ref[...], hid, preferred_element_type=jnp.float32)
            mixed = mixed - jnp.clip(mixed, -0.01, 0.01)
            parts.append(mixed.reshape(2, width, SUB, half))
        for side in range(2):
            out_ref[:, base : base + 2 * SUB, side * half : (side + 1) * half] = (
                jnp.concatenate([parts[0][side], parts[1][side]], axis=1).astype(jnp.bfloat16)
            )


def backward_kernel(x_ref, s_ref, bh_ref, swap_ref, iw_ref, out_ref):
    count, rows, cols = x_ref.shape
    mid = rows // 2
    for n in range(count):
        total = jnp.dot(bh_ref[...], s_ref[n], preferred_element_type=jnp.float32)
        plus, minus = split_rows(total, -1)
        upper = jnp.concatenate([t.astype(jnp.bfloat16) for t in plus], axis=1)
        lower = jnp.concatenate([t.astype(jnp.bfloat16) for t in minus], axis=1)
        lower = jnp.dot(swap_ref[...], lower, preferred_element_type=jnp.float32).astype(
            jnp.bfloat16
        )
        for place, part in ((0, upper), (mid, lower)):
            filtered = jnp.dot(part, iw_ref[...], preferred_element_type=jnp.float32)
            out_ref[n, place : place + mid, :] = (
                x_ref[n, place : place + mid, :].astype(jnp.float32) + filtered
            ).astype(jnp.bfloat16)


def whole_spec(array):
    zeros = (0,) * array.ndim
    return pl.BlockSpec(array.shape, lambda *_: zeros)


def per_device_local(fields, norm_gain, norm_shift, first_weight, second_weight, first_bias):
    local_ch, rows, cols = fields.shape
    half = cols // 2
    width = first_weight.shape[2]
    groups = lax.axis_size("grid")
    channels = local_ch * groups
    own_blocks = local_ch // width
    values = fields.astype(jnp.float32)
    stats = shared_stats(
        jnp.sum(values, axis=0), jnp.sum(values * values, axis=0), groups, channels
    )
    fwd_w, inv_w, low, ordered, swap = (jnp.asarray(t) for t in constant_tables(rows, cols))
    size = 2 * width * SUB
    per = 4 if local_ch % 4 == 0 else 1
    params = pltpu.CompilerParams(
        dimension_semantics=("arbitrary",), vmem_limit_bytes=60 * 1024 * 1024
    )
    image = jax.ShapeDtypeStruct(fields.shape, jnp.bfloat16)
    image_spec = pl.BlockSpec((per, rows, cols), lambda i: (i, 0, 0))
    smem = pl.BlockSpec(memory_space=pltpu.SMEM)
    cost = lambda flops: pl.CostEstimate(
        flops=flops, bytes_accessed=4 * fields.size, transcendentals=0
    )
    modes = pl.pallas_call(
        forward_kernel,
        grid=(local_ch // per,),
        out_shape=image,
        in_specs=[
            image_spec,
            whole_spec(stats),
            smem,
            smem,
            whole_spec(fwd_w),
            whole_spec(low),
        ],
        out_specs=image_spec,
        compiler_params=params,
        cost_estimate=cost(2 * fields.size * (rows + cols)),
        name="forward",
    )(fields, stats, norm_gain, norm_shift, fwd_w, low)
    depth = 8 * SUB
    mode_spec = pl.BlockSpec((width, depth, cols), lambda b, i: (b, i, 0))
    mixed = pl.pallas_call(
        mix_kernel,
        grid=(own_blocks, rows // depth),
        out_shape=image,
        in_specs=[
            mode_spec,
            whole_spec(first_weight),
            whole_spec(second_weight),
            whole_spec(first_bias),
        ],
        out_specs=mode_spec,
        scratch_shapes=[pltpu.VMEM((size, size), jnp.bfloat16)] * 2
        + [pltpu.VMEM((size, 1), jnp.float32)],
        compiler_params=pltpu.CompilerParams(
            dimension_semantics=("arbitrary", "arbitrary"), vmem_limit_bytes=60 * 1024 * 1024
        ),
        cost_estimate=cost(2 * fields.size * size),
        name="mix",
    )(modes, first_weight, second_weight, first_bias)
    return pl.pallas_call(
        backward_kernel,
        grid=(local_ch // per,),
        out_shape=image,
        in_specs=[
            image_spec,
            image_spec,
            whole_spec(ordered),
            whole_spec(swap),
            whole_spec(inv_w),
        ],
        out_specs=image_spec,
        compiler_params=params,
        cost_estimate=cost(2 * fields.size * (rows + cols)),
        name="backward",
    )(fields, mixed, ordered, swap, inv_w)


def per_device_any(fields, norm_gain, norm_shift, first_weight, second_weight, first_bias):
    local_ch, rows, cols = fields.shape
    whole_blocks = local_ch % first_weight.shape[2] == 0
    tiled = rows % 64 == 0 and cols % 256 == 0 and rows * cols <= 512 * 1024
    groups = lax.axis_size("grid")
    tiled = tiled and groups % 2 == 0 and rows % (8 * groups) == 0
    chosen = per_device_local if whole_blocks and tiled else per_device
    return chosen(fields, norm_gain, norm_shift, first_weight, second_weight, first_bias)


def solution(mesh):
    return jax.shard_map(
        per_device_any,
        mesh=mesh,
        in_specs=(P(("batch", "grid"), None, None), P(), P(), P(), P(), P()),
        out_specs=P(("batch", "grid"), None, None),
        check_vma=False,
    )
```

profile of v0, /device:TPU:0, one launch (start us, length us, event | category | flops | bytes accessed | tf_op | source)
XLA Modules:
  0.0 123.1 jit_solution(13468749125940064587)
XLA Ops:
  0.0 7.5 %fusion = (f32[512,512]{1,0:T(8,128)S(1)}, f32[512,512]{1,0:T(8,128)S(1)}) fusion(bf16[32,512,512]{2,1,0:T(8,128)(2,1)} %x_ref.3), kind=kLoop, calls=%fused_computation.2 | loop fusion | flops 33030144 | bytes 18874368 | tf_op jit(solution)/shard_map/reduce_sum | solution.py:383
  7.5 34.5 %stats.1.stats_ref = f32[2,512,512]{2,1,0:T(8,128)S(1)} custom-call(f32[512,512]{1,0:T(8,128)S(1)} %get-tuple-element.6.sum_ref, f32[512,512]{1,0:T(8,128)S(1)} %get-tuple-element.5.sq_ref), custom_call_target="tpu_custom_call" | custom-call | tf_op jit(solution)/shard_map/stats/pallas_call | solution.py:253
  42.0 0.0 copy-start
  42.0 1.3 %copy-done = f32[2,512,512]{2,1,0:T(8,128)} copy-done((f32[2,512,512]{2,1,0:T(8,128)}, f32[2,512,512]{2,1,0:T(8,128)S(1)}, u32[]{:S(2)}) %copy-start) | copy-done | bytes 2097176
  43.4 25.3 %forward.1.x_ref = bf16[32,512,512]{2,1,0:T(8,128)(2,1)} custom-call(bf16[32,512,512]{2,1,0:T(8,128)(2,1)} %x_ref.3, f32[2,512,512]{2,1,0:T(8,128)} %copy-done, f32[256]{0:T(256)} %gain_ref.1, f32[256]{0:T(256)} %shift_ref.1, bf16[512,512]{1,0:T(8,128)(2,1)} %constant.12.clone.fw_ref, bf16[512,512]{1,0:T(8,128)(2,1)} %constant.14.clone.fh_ref), custom_call_target="tpu_custom_call" | custom-call | flops 17179869184 | bytes 33554432 | tf_op jit(solution)/shard_map/forward/pallas_call | solution.py:397
  68.7 25.0 %mix.1.s_ref = bf16[32,512,512]{2,1,0:T(8,128)(2,1)} custom-call(bf16[32,512,512]{2,1,0:T(8,128)(2,1)} %forward.1.x_ref, bf16[2,8,32,32]{3,2,1,0:T(8,128)(2,1)} %first_ref.1, bf16[2,8,32,32]{3,2,1,0:T(8,128)(2,1)} %second_ref.1, f32[2,256]{1,0:T(2,128)} %bias_ref.1), custom_call_target="tpu_custom_call" | custom-call | flops 8589934592 | bytes 33554432 | tf_op jit(solution)/shard_map/mix/pallas_call | solution.py:416
  93.7 29.5 %backward.1 = bf16[32,512,512]{2,1,0:T(8,128)(2,1)} custom-call(bf16[32,512,512]{2,1,0:T(8,128)(2,1)} %x_ref.3, bf16[32,512,512]{2,1,0:T(8,128)(2,1)} %mix.1.s_ref, bf16[512,512]{1,0:T(8,128)(2,1)} %constant.15.clone.bh_ref, bf16[256,256]{1,0:T(8,128)(2,1)} %constant.16.clone.swap_ref, bf16[512,512]{1,0:T(8,128)(2,1)} %constant.13.clone.iw_ref), custom_call_target="tpu_custom_call" | custom-call | flops 17179869184 | bytes 33554432 | tf_op jit(solution)/shard_map/backward/pallas_call | solution.py:435
Async XLA Ops:
  42.0 1.4 %copy-start = (f32[2,512,512]{2,1,0:T(8,128)}, f32[2,512,512]{2,1,0:T(8,128)S(1)}, u32[]{:S(2)}) copy-start(f32[2,512,512]{2,1,0:T(8,128)S(1)} %stats.1.stats_ref) | copy-start | bytes 6291460
where the time goes:
time: 123 us
  Pallas kernels  114 us (93%)
  other arithmetic  7.54 us (6%)
  local copies, waits for them, and re-layouts  1.34 us (1%)
    pallas_call x1, Pallas kernels, shared_stats(): pl.pallas_call(functools.partial(stats_kernel, n, channels), out_shape=ja...  34.5 us
    pallas_call x1, Pallas kernels, per_device_local(): pl.pallas_call(backward_kernel, grid=(local_ch // per,), out_shape=image,...  29.5 us
    pallas_call x1, Pallas kernels, per_device_local(): pl.pallas_call(forward_kernel, grid=(local_ch // per,), out_shape=image,...  25.3 us
    pallas_call x1, Pallas kernels, per_device_local(): pl.pallas_call(mix_kernel, grid=(own_blocks, rows // depth), out_shape=im...  25 us
    reduce_sum x1, other arithmetic, per_device_local(): jnp.sum(values * values, axis=0)  7.54 us

commit v1 on v0

v1 whole, which is shorter than its diff:
```python
import functools
import math

import jax
import jax.numpy as jnp
import numpy as np
from jax import lax
from jax.experimental import pallas as pl
from jax.experimental.pallas import tpu as pltpu
from jax.sharding import PartitionSpec as P


def tables(rows, cols):
    half = cols // 2
    col_index = jnp.arange(cols, dtype=jnp.int32)
    mode_index = jnp.arange(half, dtype=jnp.int32)
    angle_w = (col_index[:, None] * mode_index[None, :] % cols).astype(jnp.float32) * (
        2.0 * math.pi / cols
    )
    scale_w = 1.0 / math.sqrt(cols)
    fwd_w = jnp.concatenate(
        [jnp.cos(angle_w) * scale_w, -jnp.sin(angle_w) * scale_w], axis=1
    ).astype(jnp.bfloat16)
    weight_k = jnp.where(mode_index == 0, 1.0, 2.0).astype(jnp.float32)
    inv_w = jnp.concatenate(
        [
            (jnp.cos(angle_w) * weight_k[None, :] * scale_w).T,
            (-jnp.sin(angle_w) * weight_k[None, :] * scale_w).T,
        ],
        axis=0,
    ).astype(jnp.bfloat16)
    row_index = jnp.arange(rows, dtype=jnp.int32)
    angle_h = (row_index[:, None] * row_index[None, :] % rows).astype(jnp.float32) * (
        2.0 * math.pi / rows
    )
    scale_h = 1.0 / math.sqrt(rows)
    cos_h = (jnp.cos(angle_h) * scale_h).astype(jnp.bfloat16)
    sin_h = (jnp.sin(angle_h) * scale_h).astype(jnp.bfloat16)
    return (fwd_w, inv_w, cos_h, sin_h)


def mult(form, left, right):
    return jnp.einsum(form, left, right, preferred_element_type=jnp.float32)


def shrink(values):
    return jnp.maximum(values - 0.01, 0.0) + jnp.minimum(values + 0.01, 0.0)


def mix_modes(real_part, imag_part, first_weight, second_weight, first_bias):
    blocks = first_weight.shape[1]
    width = first_weight.shape[2]
    shape = real_part.shape
    real_blk = real_part.reshape(blocks, width, -1)
    imag_blk = imag_part.reshape(blocks, width, -1)
    bias_blk = first_bias.reshape(2, blocks, width, 1)
    hid_re = jax.nn.relu(
        mult("bio,bim->bom", first_weight[0], real_blk)
        - mult("bio,bim->bom", first_weight[1], imag_blk)
        + bias_blk[0]
    ).astype(jnp.bfloat16)
    hid_im = jax.nn.relu(
        mult("bio,bim->bom", first_weight[0], imag_blk)
        + mult("bio,bim->bom", first_weight[1], real_blk)
        + bias_blk[1]
    ).astype(jnp.bfloat16)
    out_re = mult("bio,bim->bom", second_weight[0], hid_re) - mult(
        "bio,bim->bom", second_weight[1], hid_im
    )
    out_im = mult("bio,bim->bom", second_weight[0], hid_im) + mult(
        "bio,bim->bom", second_weight[1], hid_re
    )
    return (
        shrink(out_re).astype(jnp.bfloat16).reshape(shape),
        shrink(out_im).astype(jnp.bfloat16).reshape(shape),
    )


def per_device(fields, norm_gain, norm_shift, first_weight, second_weight, first_bias):
    local_ch, rows, cols = fields.shape
    half = cols // 2
    groups = lax.axis_size("grid")
    channels = local_ch * groups
    fwd_w, inv_w, cos_h, sin_h = tables(rows, cols)
    values = fields.astype(jnp.float32)
    start = lax.axis_index("grid") * local_ch
    gain_own = lax.dynamic_slice_in_dim(norm_gain, start, local_ch)
    shift_own = lax.dynamic_slice_in_dim(norm_shift, start, local_ch)
    total_sum, total_sq = lax.psum(
        (jnp.sum(values, axis=0), jnp.sum(values * values, axis=0)), "grid"
    )
    mean = total_sum / channels
    var = total_sq / channels - mean * mean
    normed = (
        (values - mean) * lax.rsqrt(var + 1e-05) * gain_own[:, None, None]
        + shift_own[:, None, None]
    ).astype(jnp.bfloat16)
    along_w = (
        mult("chw,wk->chk", normed, fwd_w).astype(jnp.bfloat16).reshape(local_ch, rows, 2, half)
    )
    first_p = mult("kh,chpq->ckpq", cos_h, along_w)
    first_q = mult("kh,chpq->ckpq", sin_h, along_w)
    modes = jnp.stack(
        [
            (first_p[:, :, 0] + first_q[:, :, 1]).astype(jnp.bfloat16),
            (first_p[:, :, 1] - first_q[:, :, 0]).astype(jnp.bfloat16),
        ],
        axis=2,
    )
    spread = lax.all_to_all(modes, "grid", split_axis=1, concat_axis=0, tiled=True)
    shr_re, shr_im = mix_modes(
        spread[:, :, 0], spread[:, :, 1], first_weight, second_weight, first_bias
    )
    gathered = lax.all_to_all(
        jnp.stack([shr_re, shr_im], axis=2), "grid", split_axis=0, concat_axis=1, tiled=True
    )
    back_p = mult("kh,ckpq->chpq", cos_h, gathered)
    back_q = mult("kh,ckpq->chpq", sin_h, gathered)
    back_re = (back_p[:, :, 0] - back_q[:, :, 1]).astype(jnp.bfloat16)
    back_im = (back_p[:, :, 1] + back_q[:, :, 0]).astype(jnp.bfloat16)
    backed = jnp.concatenate([back_re, back_im], axis=2)
    filtered = mult("chk,kw->chw", backed, inv_w)
    return (values + filtered).astype(jnp.bfloat16)

SUB = 8


def stats_kernel(n, channels, sum_ref, sq_ref, out_ref, near, part, far, s1, r1, s2, r2, s3, r3, s4, r4):
    me = lax.axis_index("grid")
    chips = n // 2
    core, chip = lax.rem(me, 2), lax.div(me, 2)
    other = 1 - core
    sibling = chip * 2 + other
    rows = sum_ref.shape[0]
    half, piece = rows // 2, rows // n

    def ahead(j):
        return lax.rem(chip + j, chips)

    def span(c, k):
        return pl.ds(pl.multiple_of(c * half + k * piece, 8), piece)

    def send(source, target, send_sem, recv_sem, device):
        copy = pltpu.make_async_remote_copy(
            src_ref=source,
            dst_ref=target,
            send_sem=send_sem,
            recv_sem=recv_sem,
            device_id={"grid": device},
            device_id_type=pl.DeviceIdType.MESH,
        )
        copy.start()
        return copy

    barrier = pltpu.get_barrier_semaphore()
    for device in [sibling] + [ahead(j) * 2 + core for j in range(1, chips)]:
        pl.semaphore_signal(
            barrier, inc=1, device_id={"grid": device}, device_id_type=pl.DeviceIdType.MESH
        )
    pl.semaphore_wait(barrier, chips)

    theirs = pl.ds(pl.multiple_of(other * half, 8), half)
    first = [
        send(ref.at[theirs], near.at[i], s1.at[i], r1.at[i], sibling)
        for i, ref in enumerate((sum_ref, sq_ref))
    ]
    for copy in first:
        copy.wait_recv()
    second = []
    for j in range(1, chips + 1):
        k = ahead(j)
        local = pl.ds(pl.multiple_of(k * piece, 8), piece)
        for i, ref in enumerate((sum_ref, sq_ref)):
            part[j - 1, i] = ref[span(core, k)] + near[i, local]
    for j in range(1, chips):
        second.append(
            send(part.at[j - 1], far.at[j - 1], s2.at[j - 1], r2.at[j - 1], ahead(j) * 2 + core)
        )
    total_sum, total_sq = part[chips - 1, 0], part[chips - 1, 1]
    for j in range(1, chips):
        second[j - 1].wait_recv()
        total_sum = total_sum + far[j - 1, 0]
        total_sq = total_sq + far[j - 1, 1]
    mean = total_sum * (1.0 / channels)
    mine = span(core, chip)
    out_ref[0, mine] = mean
    out_ref[1, mine] = lax.rsqrt(total_sq * (1.0 / channels) - mean * mean + 1e-05)
    block = out_ref.at[:, mine]
    third = [
        send(block, block, s3.at[j - 1], r3.at[j - 1], ahead(j) * 2 + core)
        for j in range(1, chips)
    ]
    fourth = [send(block, block, s4.at[0], r4.at[0], sibling)]
    for j in range(1, chips):
        third[j - 1].wait_recv()
        block = out_ref.at[:, span(core, ahead(chips - j))]
        fourth.append(send(block, block, s4.at[j], r4.at[j], sibling))
    for copy in fourth:
        copy.wait_recv()
    for copy in first + second + third + fourth:
        copy.wait_send()


def shared_stats(total_sum, total_sq, n, channels):
    rows, cols = total_sum.shape
    chips = n // 2
    vmem = pl.BlockSpec(memory_space=pltpu.VMEM)
    counts = (2, chips - 1, chips - 1, chips)
    return pl.pallas_call(
        functools.partial(stats_kernel, n, channels),
        out_shape=jax.ShapeDtypeStruct((2, rows, cols), jnp.float32),
        in_specs=[vmem, vmem],
        out_specs=vmem,
        scratch_shapes=[
            pltpu.VMEM((2, rows // 2, cols), jnp.float32),
            pltpu.VMEM((chips, 2, rows // n, cols), jnp.float32),
            pltpu.VMEM((chips - 1, 2, rows // n, cols), jnp.float32),
        ]
        + [pltpu.SemaphoreType.DMA((c,)) for c in counts for _ in range(2)],
        compiler_params=pltpu.CompilerParams(
            collective_id=0, has_side_effects=True, vmem_limit_bytes=32 * 1024 * 1024
        ),
        name="stats",
    )(total_sum, total_sq)


LANE = 128
SETS = 4


def wave(f, left, right, period):
    return f(
        (left[:, None] * right[None, :] % period).astype(np.float32)
        * np.float32(2.0 * math.pi / period)
    ) * np.float32(1.0 / math.sqrt(period))


def split_tables(rows, cols):
    half_r, half_c = rows // 2, cols // 2
    col, mode = np.arange(half_c), 2 * np.arange(half_c // 2)
    fwd, inv = [], []
    for odd in range(2):
        cos_w, sin_w = (wave(f, col, mode + odd, cols) for f in (np.cos, np.sin))
        fwd.append(np.concatenate([cos_w, -sin_w], axis=1))
        weight = np.where(mode + odd == 0, 1.0, 2.0).astype(np.float32)[:, None]
        inv.append(np.concatenate([cos_w.T * weight, -sin_w.T * weight], axis=0))
    row, pair = np.arange(half_r), 2 * np.arange(rows // 4)
    turn = []
    for odd in range(2):
        cos_h, sin_h = (wave(f, pair + odd, row, rows) for f in (np.cos, np.sin))
        on_re, on_im = [cos_h, -sin_h], [sin_h, cos_h]
        if odd == 0:
            middle = wave(np.cos, np.array([half_r]), row, rows)[0]
            on_re[1][0] = middle
            on_im[0] = on_im[0].copy()
            on_im[0][0] = middle
        for parts in (on_re, on_im):
            blocks = [p.reshape(-1, SETS, half_r) for p in parts]
            turn.append(np.concatenate(blocks, axis=1).reshape(half_r, half_r))
    turn = np.stack(turn)
    tables = (np.stack(fwd), turn, turn.transpose(0, 2, 1), np.stack(inv))
    return tuple(np.ascontiguousarray(t).astype(jnp.bfloat16) for t in tables)


def normal_modes(x_ref, stats_ref, n, scale, fwd_ref, turn_ref, lift):
    rows, cols = x_ref.shape[1:]
    half_r, half_c = rows // 2, cols // 2
    quarter = half_c // 2
    values = x_ref[n].astype(jnp.float32)
    normed = ((values - stats_ref[0]) * stats_ref[1] * scale).astype(jnp.bfloat16)
    left, right = normed[:, :half_c], normed[:, half_c:]
    along = [
        jnp.dot(part, fwd_ref[i], preferred_element_type=jnp.float32).astype(jnp.bfloat16)
        for i, part in enumerate((left + right, left - right))
    ]
    along = [
        jnp.concatenate([a[:, p * quarter : (p + 1) * quarter] for a in along], axis=1)
        for p in range(2)
    ]
    out = []
    for odd in range(2):
        turned = []
        for p in range(2):
            top, low = along[p][:half_r], along[p][half_r:]
            part = top - low if odd else top + low
            turned.append(
                jnp.dot(turn_ref[2 * odd + p], part, preferred_element_type=jnp.float32)
            )
        plus, minus = turned[0] + turned[1], turned[0] - turned[1]
        if odd == 0:
            first, second = turned[0][:SUB], turned[1][:SUB]
            line = lax.broadcasted_iota(jnp.int32, first.shape, 0)
            lane = lax.broadcasted_iota(jnp.int32, first.shape, 1)
            head = jnp.where(line == 0, first, jnp.where(line == SETS, second, plus[:SUB]))
            head = head + jnp.where((line == 0) & (lane == 0), lift, 0.0)
            tail = jnp.where(
                line == 0,
                pltpu.roll(first, SETS, 0),
                jnp.where(line == SETS, -pltpu.roll(second, SETS, 0), minus[:SUB]),
            )
            plus = jnp.concatenate([head, plus[SUB:]], axis=0)
            minus = jnp.concatenate([tail, minus[SUB:]], axis=0)
        out += [plus, minus]
    return out


def wide_weight(real, imag, flip_in, flip_out):
    size = real.shape[0]
    rows = lax.broadcasted_iota(jnp.int32, (size * SUB, size), 0)
    cols = lax.broadcasted_iota(jnp.int32, (size * SUB, size), 1)
    repeat = jnp.where((rows >= cols * SUB) & (rows < cols * SUB + SUB), 1.0, 0.0).astype(
        jnp.bfloat16
    )
    last = (((1,), (1,)), ((), ()))
    full = []
    for weight in (real, imag):
        tall = lax.dot_general(repeat, weight, last, preferred_element_type=jnp.float32)
        full.append(
            lax.dot_general(
                tall.astype(jnp.bfloat16), repeat, last, preferred_element_type=jnp.float32
            )
        )
    left = lax.broadcasted_iota(jnp.int32, full[0].shape, 0)
    right = lax.broadcasted_iota(jnp.int32, full[0].shape, 1)
    same = ((left ^ right) & (SETS - 1)) == 0
    im_out, im_in = (left & SETS) != 0, (right & SETS) != 0
    value = jnp.where(
        im_out, jnp.where(im_in, full[0], full[1]), jnp.where(im_in, -full[1], full[0])
    )
    value = jnp.where(same, value, 0.0)
    flips = []
    for flip_i, flip_o in ((False, False), (flip_in, flip_out)):
        turned = jnp.where(im_in, -value, value) if flip_i else value
        flips.append(jnp.where(im_out, -turned, turned) if flip_o else turned)
    return [f.astype(jnp.bfloat16) for f in flips]


def prepare(block, first_ref, second_ref, bias_ref, w_ref, b1_ref):
    width = first_ref.shape[2]
    size = width * SUB
    for i, (source, flip) in enumerate(((first_ref, True), (second_ref, False))):
        pair = wide_weight(source[0, block], source[1, block], flip, not flip)
        for j in range(2):
            w_ref[2 * i + j] = pair[j]
    shape = (size, bias_ref.shape[1])
    line = lax.broadcasted_iota(jnp.int32, shape, 0)
    offset = line - (lax.broadcasted_iota(jnp.int32, shape, 1) - block * width) * SUB
    own = (offset >= 0) & (offset < SUB)
    picked = jnp.where((line & SETS) == 0, bias_ref[0:1, :], bias_ref[1:2, :])
    column = jnp.sum(jnp.where(own, picked, 0.0), axis=1, keepdims=True)
    b1_ref[...] = jnp.broadcast_to(column, b1_ref.shape)


def mix_pair(a_ref, b_ref, w_ref, b1_ref, odd, start, groups, edge):
    width = b_ref.shape[0]
    cols = b_ref.shape[3]
    sums, gaps = [], []
    for g in range(2):
        mixed = []
        for side in range(2):
            values = a_ref[(2 * odd + side) * groups + start + g]
            hid = jnp.dot(w_ref[side], values, preferred_element_type=jnp.float32)
            hid = (hid + b1_ref[...]).astype(jnp.bfloat16)
            hid = jnp.maximum(hid, jnp.zeros_like(hid))
            out = jnp.dot(w_ref[2 + side], hid, preferred_element_type=jnp.float32)
            mixed.append((out - jnp.clip(out, -0.01, 0.01)).reshape(width, SUB, cols))
        total, gap = mixed[0] + mixed[1], mixed[0] - mixed[1]
        if edge is not None and g == 0:
            line = lax.broadcasted_iota(jnp.int32, total.shape, 1)
            moved = pltpu.roll(mixed[1], SETS, 1)
            re_edge, im_edge = (line == 0) & edge, (line == SETS) & edge
            total = jnp.where(re_edge, mixed[0], jnp.where(im_edge, moved, total))
            gap = jnp.where(re_edge, -moved, jnp.where(im_edge, mixed[0], gap))
        sums.append(total)
        gaps.append(gap)
    spot = pl.ds(pl.multiple_of(start * SUB, 2 * SUB), 2 * SUB)
    for i, parts in enumerate((sums, gaps)):
        b_ref[:, 2 * odd + i, spot, :] = jnp.concatenate(parts, axis=1).astype(jnp.bfloat16)


def return_rows(x_ref, n, b_ref, channel, back_ref, inv_ref, out_ref):
    rows, cols = x_ref.shape[1:]
    half_c = cols // 2
    quarter = half_c // 2
    parts = []
    for p in range(2):
        even, odd = (
            jnp.dot(back_ref[2 * i + p], b_ref[channel, 2 * i + p], preferred_element_type=jnp.float32)
            for i in range(2)
        )
        parts.append(jnp.concatenate([even + odd, even - odd], axis=0).astype(jnp.bfloat16))
    even, odd = (
        jnp.dot(
            jnp.concatenate([t[:, i * quarter : (i + 1) * quarter] for t in parts], axis=1),
            inv_ref[i],
            preferred_element_type=jnp.float32,
        )
        for i in range(2)
    )
    for i, filtered in enumerate((even + odd, even - odd)):
        span = slice(i * half_c, (i + 1) * half_c)
        out_ref[n, :, span] = (x_ref[n, :, span].astype(jnp.float32) + filtered).astype(
            jnp.bfloat16
        )


def main_kernel(
    plan,
    x_ref,
    stats_ref,
    gain_ref,
    shift_ref,
    first_ref,
    second_ref,
    bias_ref,
    fwd_ref,
    turn_ref,
    back_ref,
    inv_ref,
    out_ref,
    a_ref,
    b_ref,
    w_ref,
    b1_ref,
):
    steps, mixes, minis = plan
    step = pl.program_id(0)
    count, rows, cols = x_ref.shape
    half_r = rows // 2
    groups = half_r // SUB
    width = first_ref.shape[2]
    index = lax.axis_index("grid")

    @pl.when(step == 0)
    def _():
        prepare(index, first_ref, second_ref, bias_ref, w_ref, b1_ref)

    @pl.when(step < steps)
    def _():
        here = step * count
        lift_scale = float(cols * rows) * float(fwd_first(cols)) * float(fwd_first(rows))
        for n in range(0, count, 2):
            pair = [
                normal_modes(
                    x_ref,
                    stats_ref,
                    n + i,
                    gain_ref[index * width + here + n + i],
                    fwd_ref,
                    turn_ref,
                    shift_ref[index * width + here + n + i] * lift_scale,
                )
                for i in range(2)
            ]
            spot = pl.ds(pl.multiple_of((here + n) * SUB, 2 * SUB), 2 * SUB)
            for kind in range(4):
                both = [p[kind].reshape(groups, SUB, -1) for p in pair]
                a_ref[kind * groups : (kind + 1) * groups, spot, :] = jnp.concatenate(
                    both, axis=1
                ).astype(jnp.bfloat16)

    @pl.when((step >= steps) & (step < steps + mixes))
    def _():
        now = step - steps
        for u in range(minis):
            mini = now * minis + u
            odd, start = lax.div(mini, groups // 2), 2 * lax.rem(mini, groups // 2)
            mix_pair(
                a_ref, b_ref, w_ref, b1_ref, odd, start, groups, now == 0 if u == 0 else None
            )

    @pl.when(step >= steps + mixes)
    def _():
        here = (step - steps - mixes) * count
        for n in range(count):
            return_rows(x_ref, n, b_ref, here + n, back_ref, inv_ref, out_ref)


def fwd_first(size):
    return np.asarray(np.float32(1.0 / math.sqrt(size))).astype(jnp.bfloat16).astype(np.float32)


def whole_spec(array):
    zeros = (0,) * array.ndim
    return pl.BlockSpec(array.shape, lambda *_: zeros)


def mix_tokens(fields, stats, norm_gain, norm_shift, first_weight, second_weight, first_bias):
    local_ch, rows, cols = fields.shape
    half_r, half_c = rows // 2, cols // 2
    tables = [jnp.asarray(t) for t in split_tables(rows, cols)]
    size = first_weight.shape[2] * SUB
    per = 4 if local_ch % 4 == 0 else 2
    steps = local_ch // per
    minis = 4
    mixes = half_r // SUB // minis
    image = jax.ShapeDtypeStruct(fields.shape, jnp.bfloat16)
    last = steps - 1
    x_spec = pl.BlockSpec(
        (per, rows, cols),
        lambda i: (jnp.where(i < steps, i, jnp.maximum(i - steps - mixes, 0)), 0, 0),
    )
    out_spec = pl.BlockSpec(
        (per, rows, cols), lambda i: (jnp.maximum(i - steps - mixes, 0), 0, 0)
    )
    smem = pl.BlockSpec(memory_space=pltpu.SMEM)
    return pl.pallas_call(
        functools.partial(main_kernel, (steps, mixes, minis)),
        grid=(2 * steps + mixes,),
        out_shape=image,
        in_specs=[x_spec, whole_spec(stats), smem, smem]
        + [whole_spec(t) for t in (first_weight, second_weight, first_bias, *tables)],
        out_specs=out_spec,
        scratch_shapes=[
            pltpu.VMEM((4 * half_r // SUB, size, half_c), jnp.bfloat16),
            pltpu.VMEM((local_ch, 4, half_r, half_c), jnp.bfloat16),
            pltpu.VMEM((4, size, size), jnp.bfloat16),
            pltpu.VMEM((size, half_c), jnp.float32),
        ],
        compiler_params=pltpu.CompilerParams(
            dimension_semantics=("arbitrary",), vmem_limit_bytes=64 * 1000 * 1000
        ),
        cost_estimate=pl.CostEstimate(
            flops=6 * fields.size * rows, bytes_accessed=6 * fields.size, transcendentals=0
        ),
        name="main",
    )(fields, stats, norm_gain, norm_shift, first_weight, second_weight, first_bias, *tables)


def per_device_local(fields, norm_gain, norm_shift, first_weight, second_weight, first_bias):
    groups = lax.axis_size("grid")
    values = fields.astype(jnp.float32)
    stats = shared_stats(
        jnp.sum(values, axis=0),
        jnp.sum(values * values, axis=0),
        groups,
        fields.shape[0] * groups,
    )
    return mix_tokens(
        fields, stats, norm_gain, norm_shift, first_weight, second_weight, first_bias
    )


def per_device_any(fields, norm_gain, norm_shift, first_weight, second_weight, first_bias):
    local_ch, rows, cols = fields.shape
    groups = lax.axis_size("grid")
    one_block = local_ch == first_weight.shape[2] and local_ch % 2 == 0
    tiled = rows % 256 == 0 and cols % 512 == 0 and local_ch * rows * cols <= 8 * 1024 * 1024
    tiled = tiled and groups % 2 == 0 and rows % (8 * groups) == 0
    chosen = per_device_local if one_block and tiled else per_device
    return chosen(fields, norm_gain, norm_shift, first_weight, second_weight, first_bias)


def solution(mesh):
    return jax.shard_map(
        per_device_any,
        mesh=mesh,
        in_specs=(P(("batch", "grid"), None, None), P(), P(), P(), P(), P()),
        out_specs=P(("batch", "grid"), None, None),
        check_vma=False,
    )
```

time: 123 us -> 93.2 us (0.76)
  Pallas kernels: 114 us -> 84 us
    pallas_call x3 -> x1, Pallas kernels: 79.8 us -> 49.5 us  [mix_tokens(): pl.pallas_call(functools.partial(main_kernel, (steps, mixes, minis)), gri...]
where the time goes in v1:
time: 93.2 us; the launch traced here: 92.9 us
  Pallas kernels  84 us (90%)
  other arithmetic  7.54 us (8%)
  local copies, waits for them, and re-layouts  1.34 us (1%)
    pallas_call x1, Pallas kernels, mix_tokens(): pl.pallas_call(functools.partial(main_kernel, (steps, mixes, minis)), gri...  49.5 us
    pallas_call x1, Pallas kernels, shared_stats(): pl.pallas_call(functools.partial(stats_kernel, n, channels), out_shape=ja...  34.5 us
    reduce_sum x1, other arithmetic, per_device_local(): jnp.sum(values * values, axis=0)  7.54 us

profile of v1, /device:TPU:0, one launch (start us, length us, event | category | flops | bytes accessed | tf_op | source)
XLA Modules:
  0.0 92.9 jit_solution(11926381250070151366)
XLA Ops:
  0.0 7.5 %fusion = (f32[512,512]{1,0:T(8,128)S(1)}, f32[512,512]{1,0:T(8,128)S(1)}) fusion(bf16[32,512,512]{2,1,0:T(8,128)(2,1)} %x_ref.1), kind=kLoop, calls=%fused_computation.2 | loop fusion | flops 33030144 | bytes 18874368 | tf_op jit(solution)/shard_map/reduce_sum | solution.py:535
  7.5 34.5 %stats.1.stats_ref = f32[2,512,512]{2,1,0:T(8,128)S(1)} custom-call(f32[512,512]{1,0:T(8,128)S(1)} %get-tuple-element.6.sum_ref, f32[512,512]{1,0:T(8,128)S(1)} %get-tuple-element.5.sq_ref), custom_call_target="tpu_custom_call" | custom-call | tf_op jit(solution)/shard_map/stats/pallas_call | solution.py:209
  42.0 0.0 copy-start
  42.0 1.3 %copy-done = f32[2,512,512]{2,1,0:T(8,128)} copy-done((f32[2,512,512]{2,1,0:T(8,128)}, f32[2,512,512]{2,1,0:T(8,128)S(1)}, u32[]{:S(2)}) %copy-start) | copy-done | bytes 2097176
  43.4 49.5 %main.1 = bf16[32,512,512]{2,1,0:T(8,128)(2,1)} custom-call(bf16[32,512,512]{2,1,0:T(8,128)(2,1)} %x_ref.1, f32[2,512,512]{2,1,0:T(8,128)} %copy-done, f32[256]{0:T(256)} %gain_ref.1, f32[256]{0:T(256)} %shift_ref.1, bf16[2,8,32,32]{3,2,1,0:T(8,128)(2,1)} %first_ref.1, bf16[2,8,32,32]{3,2,1,0:T(8,128)(2,1)} %second_ref.1, f32[2,256]{1,0:T(2,128)} %bias_ref.1, ...), custom_call_target="tpu_custom_call" | custom-call | flops 25769803776 | bytes 50331648 | tf_op jit(solution)/shard_map/main/pallas_call | solution.py:507
Async XLA Ops:
  42.0 1.4 %copy-start = (f32[2,512,512]{2,1,0:T(8,128)}, f32[2,512,512]{2,1,0:T(8,128)S(1)}, u32[]{:S(2)}) copy-start(f32[2,512,512]{2,1,0:T(8,128)S(1)} %stats.1.stats_ref) | copy-start | bytes 6291460

commit v2 on v1

--- a/solution.py
+++ b/solution.py
@@ -123,105 +123,6 @@
     return (values + filtered).astype(jnp.bfloat16)
 
 SUB = 8
-
-
-def stats_kernel(n, channels, sum_ref, sq_ref, out_ref, near, part, far, s1, r1, s2, r2, s3, r3, s4, r4):
-    me = lax.axis_index("grid")
-    chips = n // 2
-    core, chip = lax.rem(me, 2), lax.div(me, 2)
-    other = 1 - core
-    sibling = chip * 2 + other
-    rows = sum_ref.shape[0]
-    half, piece = rows // 2, rows // n
-
-    def ahead(j):
-        return lax.rem(chip + j, chips)
-
-    def span(c, k):
-        return pl.ds(pl.multiple_of(c * half + k * piece, 8), piece)
-
-    def send(source, target, send_sem, recv_sem, device):
-        copy = pltpu.make_async_remote_copy(
-            src_ref=source,
-            dst_ref=target,
-            send_sem=send_sem,
-            recv_sem=recv_sem,
-            device_id={"grid": device},
-            device_id_type=pl.DeviceIdType.MESH,
-        )
-        copy.start()
-        return copy
-
-    barrier = pltpu.get_barrier_semaphore()
-    for device in [sibling] + [ahead(j) * 2 + core for j in range(1, chips)]:
-        pl.semaphore_signal(
-            barrier, inc=1, device_id={"grid": device}, device_id_type=pl.DeviceIdType.MESH
-        )
-    pl.semaphore_wait(barrier, chips)
-
-    theirs = pl.ds(pl.multiple_of(other * half, 8), half)
-    first = [
-        send(ref.at[theirs], near.at[i], s1.at[i], r1.at[i], sibling)
-        for i, ref in enumerate((sum_ref, sq_ref))
-    ]
-    for copy in first:
-        copy.wait_recv()
-    second = []
-    for j in range(1, chips + 1):
-        k = ahead(j)
-        local = pl.ds(pl.multiple_of(k * piece, 8), piece)
-        for i, ref in enumerate((sum_ref, sq_ref)):
-            part[j - 1, i] = ref[span(core, k)] + near[i, local]
-    for j in range(1, chips):
-        second.append(
-            send(part.at[j - 1], far.at[j - 1], s2.at[j - 1], r2.at[j - 1], ahead(j) * 2 + core)
-        )
-    total_sum, total_sq = part[chips - 1, 0], part[chips - 1, 1]
-    for j in range(1, chips):
-        second[j - 1].wait_recv()
-        total_sum = total_sum + far[j - 1, 0]
-        total_sq = total_sq + far[j - 1, 1]
-    mean = total_sum * (1.0 / channels)
-    mine = span(core, chip)
-    out_ref[0, mine] = mean
-    out_ref[1, mine] = lax.rsqrt(total_sq * (1.0 / channels) - mean * mean + 1e-05)
-    block = out_ref.at[:, mine]
-    third = [
-        send(block, block, s3.at[j - 1], r3.at[j - 1], ahead(j) * 2 + core)
-        for j in range(1, chips)
-    ]
-    fourth = [send(block, block, s4.at[0], r4.at[0], sibling)]
-    for j in range(1, chips):
-        third[j - 1].wait_recv()
-        block = out_ref.at[:, span(core, ahead(chips - j))]
-        fourth.append(send(block, block, s4.at[j], r4.at[j], sibling))
-    for copy in fourth:
-        copy.wait_recv()
-    for copy in first + second + third + fourth:
-        copy.wait_send()
-
-
-def shared_stats(total_sum, total_sq, n, channels):
-    rows, cols = total_sum.shape
-    chips = n // 2
-    vmem = pl.BlockSpec(memory_space=pltpu.VMEM)
-    counts = (2, chips - 1, chips - 1, chips)
-    return pl.pallas_call(
-        functools.partial(stats_kernel, n, channels),
-        out_shape=jax.ShapeDtypeStruct((2, rows, cols), jnp.float32),
-        in_specs=[vmem, vmem],
-        out_specs=vmem,
-        scratch_shapes=[
-            pltpu.VMEM((2, rows // 2, cols), jnp.float32),
-            pltpu.VMEM((chips, 2, rows // n, cols), jnp.float32),
-            pltpu.VMEM((chips - 1, 2, rows // n, cols), jnp.float32),
-        ]
-        + [pltpu.SemaphoreType.DMA((c,)) for c in counts for _ in range(2)],
-        compiler_params=pltpu.CompilerParams(
-            collective_id=0, has_side_effects=True, vmem_limit_bytes=32 * 1024 * 1024
-        ),
-        name="stats",
-    )(total_sum, total_sq)
 
 
 LANE = 128
@@ -262,19 +163,18 @@
     return tuple(np.ascontiguousarray(t).astype(jnp.bfloat16) for t in tables)
 
 
-def normal_modes(x_ref, stats_ref, n, scale, fwd_ref, turn_ref, lift):
-    rows, cols = x_ref.shape[1:]
+def turn_rows(along_ref, n, turn_ref, lift):
+    rows, cols = along_ref.shape[1:]
     half_r, half_c = rows // 2, cols // 2
     quarter = half_c // 2
-    values = x_ref[n].astype(jnp.float32)
-    normed = ((values - stats_ref[0]) * stats_ref[1] * scale).astype(jnp.bfloat16)
-    left, right = normed[:, :half_c], normed[:, half_c:]
     along = [
-        jnp.dot(part, fwd_ref[i], preferred_element_type=jnp.float32).astype(jnp.bfloat16)
-        for i, part in enumerate((left + right, left - right))
-    ]
-    along = [
-        jnp.concatenate([a[:, p * quarter : (p + 1) * quarter] for a in along], axis=1)
+        jnp.concatenate(
+            [
+                along_ref[n, :, i * half_c + p * quarter : i * half_c + (p + 1) * quarter]
+                for i in range(2)
+            ],
+            axis=1,
+        )
         for p in range(2)
     ]
     out = []
@@ -351,6 +251,261 @@
     b1_ref[...] = jnp.broadcast_to(column, b1_ref.shape)
 
 
+CHUNKS = 4
+TOGETHER = 4
+
+
+def token_kernel(
+    n,
+    x_hbm,
+    gain_ref,
+    fwd_ref,
+    along_hbm,
+    x_ref,
+    sums,
+    stats,
+    near,
+    part_s,
+    part_m,
+    far_s,
+    far_m,
+    ag_out,
+    ag_in,
+    stage,
+    load_sem,
+    store_sem,
+    s1,
+    r1,
+    s2,
+    r2,
+    s3,
+    r3,
+    s4,
+    r4,
+):
+    me = lax.axis_index("grid")
+    chips = n // 2
+    core, chip = lax.rem(me, 2), lax.div(me, 2)
+    sibling = chip * 2 + 1 - core
+    local_ch, rows, cols = x_ref.shape
+    half_c = cols // 2
+    height = rows // CHUNKS
+    half, piece = height // 2, height // n
+    share = 2.0 * local_ch
+
+    def ahead(j):
+        return lax.rem(chip + j, chips)
+
+    def span(c, owner, k):
+        return pl.ds(pl.multiple_of(c * height + owner * half + k * piece, piece), piece)
+
+    def halves(c, owner):
+        return pl.ds(pl.multiple_of(c * height + owner * half, half), half)
+
+    def send(source, target, send_sem, recv_sem, device):
+        copy = pltpu.make_async_remote_copy(
+            src_ref=source,
+            dst_ref=target,
+            send_sem=send_sem,
+            recv_sem=recv_sem,
+            device_id={"grid": device},
+            device_id_type=pl.DeviceIdType.MESH,
+        )
+        copy.start()
+        return copy
+
+    loads = [
+        pltpu.make_async_copy(
+            x_hbm.at[:, c * height : (c + 1) * height],
+            x_ref.at[:, c * height : (c + 1) * height],
+            load_sem.at[c],
+        )
+        for c in range(CHUNKS)
+    ]
+    for copy in loads:
+        copy.start()
+    barrier = pltpu.get_barrier_semaphore()
+    for device in [sibling] + [ahead(j) * 2 + core for j in range(1, chips)]:
+        pl.semaphore_signal(
+            barrier, inc=1, device_id={"grid": device}, device_id_type=pl.DeviceIdType.MESH
+        )
+
+    first, second, third, fourth, stores = {}, {}, {}, {}, {}
+
+    def add_local(c):
+        loads[c].wait()
+        lines = 2 * SUB
+
+        def body(r, carry):
+            at = pl.ds(pl.multiple_of(c * height + r * lines, lines), lines)
+            total = jnp.zeros((lines, cols), jnp.float32)
+            square = jnp.zeros((lines, cols), jnp.float32)
+            for ch in range(local_ch):
+                value = x_ref[ch, at, :].astype(jnp.float32)
+                total = total + value
+                square = square + value * value
+            sums[0, at, :] = total
+            sums[1, at, :] = square
+            return carry
+
+        lax.fori_loop(0, height // lines, body, 0)
+        if c == 0:
+            pl.semaphore_wait(barrier, chips)
+        first[c] = send(
+            sums.at[:, halves(c, 1 - core)], near.at[c], s1.at[c], r1.at[c], sibling
+        )
+
+    def add_chip(c):
+        first[c].wait_recv()
+        for j in range(1, chips + 1):
+            k = ahead(j)
+            local = pl.ds(pl.multiple_of(k * piece, piece), piece)
+            total = sums[0, span(c, core, k)] + near[c, 0, local]
+            square = sums[1, span(c, core, k)] + near[c, 1, local]
+            part_s[c, j - 1] = total
+            part_m[c, j - 1] = (square - total * total * (1.0 / share)).astype(jnp.bfloat16)
+        second[c] = []
+        for j in range(1, chips):
+            device = ahead(j) * 2 + core
+            for i, (source, target) in enumerate(((part_s, far_s), (part_m, far_m))):
+                at = (c * (chips - 1) + j - 1) * 2 + i
+                second[c].append(
+                    send(source.at[c, j - 1], target.at[c, j - 1], s2.at[at], r2.at[at], device)
+                )
+
+    def finish(c):
+        for copy in second[c]:
+            copy.wait_recv()
+        own = part_s[c, chips - 1]
+        others = [far_s[c, j] for j in range(chips - 1)]
+        total = own
+        for other in others:
+            total = total + other
+        mean = total * (1.0 / (share * chips))
+        spread = part_m[c, chips - 1].astype(jnp.float32)
+        for j in range(chips - 1):
+            spread = spread + far_m[c, j].astype(jnp.float32)
+        gaps = [mean - other * (1.0 / share) for other in others]
+        for gap in gaps + [mean - own * (1.0 / share)]:
+            spread = spread + gap * gap * share
+        scale = lax.rsqrt(spread * (1.0 / (share * chips)) + 1e-05)
+        mine = span(c, core, chip)
+        stats[0, mine] = mean
+        stats[1, mine] = scale
+        third[c] = []
+        for j in range(1, chips):
+            ag_out[c, j - 1, 0] = gaps[j - 1].astype(jnp.bfloat16)
+            ag_out[c, j - 1, 1] = scale.astype(jnp.bfloat16)
+        for j in range(1, chips):
+            at = c * (chips - 1) + j - 1
+            third[c].append(
+                send(
+                    ag_out.at[c, j - 1],
+                    ag_in.at[c, j - 1],
+                    s3.at[at],
+                    r3.at[at],
+                    ahead(chips - j) * 2 + core,
+                )
+            )
+
+    def collect(c):
+        for copy in third[c]:
+            copy.wait_recv()
+        for j in range(1, chips):
+            at = span(c, core, ahead(j))
+            gap = ag_in[c, j - 1, 0].astype(jnp.float32)
+            stats[0, at] = part_s[c, j - 1] * (1.0 / share) + gap
+            stats[1, at] = ag_in[c, j - 1, 1].astype(jnp.float32)
+        block = stats.at[:, halves(c, core)]
+        fourth[c] = send(block, block, s4.at[c], r4.at[c], sibling)
+
+    def transform(c):
+        fourth[c].wait_recv()
+        slot = c % 2
+        if c >= 2:
+            stores[c - 2].wait()
+        at = slice(c * height, (c + 1) * height)
+
+        def body(i, carry):
+            sides = [[], []]
+            for u in range(TOGETHER):
+                ch = i * TOGETHER + u
+                value = x_ref[ch, at, :].astype(jnp.float32)
+                gain = gain_ref[me * local_ch + ch]
+                normed = ((value - stats[0, at, :]) * stats[1, at, :] * gain).astype(
+                    jnp.bfloat16
+                )
+                left, right = normed[:, :half_c], normed[:, half_c:]
+                sides[0].append(left + right)
+                sides[1].append(left - right)
+            for side in range(2):
+                along = jnp.dot(
+                    jnp.concatenate(sides[side], axis=0),
+                    fwd_ref[side],
+                    preferred_element_type=jnp.float32,
+                )
+                stage[
+                    slot, pl.ds(i * TOGETHER, TOGETHER), :, side * half_c : (side + 1) * half_c
+                ] = along.reshape(TOGETHER, height, half_c).astype(jnp.bfloat16)
+            return carry
+
+        lax.fori_loop(0, local_ch // TOGETHER, body, 0)
+        stores[c] = pltpu.make_async_copy(
+            stage.at[slot], along_hbm.at[:, at], store_sem.at[slot]
+        )
+        stores[c].start()
+
+    stages = (add_local, add_chip, finish, collect, transform)
+    for tick in range(CHUNKS + len(stages) - 1):
+        for depth, stage_of in enumerate(stages):
+            if 0 <= tick - depth < CHUNKS:
+                stage_of(tick - depth)
+    for c in range(max(CHUNKS - 2, 0), CHUNKS):
+        stores[c].wait()
+    for c in range(CHUNKS):
+        for copy in [first[c], fourth[c]] + second[c] + third[c]:
+            copy.wait_send()
+
+
+def token_rows(fields, norm_gain, fwd, n):
+    local_ch, rows, cols = fields.shape
+    chips = n // 2
+    height = rows // CHUNKS
+    half, piece = height // 2, height // n
+    counts = (CHUNKS, CHUNKS * (chips - 1) * 2, CHUNKS * (chips - 1), CHUNKS)
+    f32, bf16 = jnp.float32, jnp.bfloat16
+    return pl.pallas_call(
+        functools.partial(token_kernel, n),
+        out_shape=jax.ShapeDtypeStruct(fields.shape, bf16),
+        in_specs=[
+            pl.BlockSpec(memory_space=pl.ANY),
+            pl.BlockSpec(memory_space=pltpu.SMEM),
+            pl.BlockSpec(memory_space=pltpu.VMEM),
+        ],
+        out_specs=pl.BlockSpec(memory_space=pl.ANY),
+        scratch_shapes=[
+            pltpu.VMEM(fields.shape, bf16),
+            pltpu.VMEM((2, rows, cols), f32),
+            pltpu.VMEM((2, rows, cols), f32),
+            pltpu.VMEM((CHUNKS, 2, half, cols), f32),
+            pltpu.VMEM((CHUNKS, chips, piece, cols), f32),
+            pltpu.VMEM((CHUNKS, chips, piece, cols), bf16),
+            pltpu.VMEM((CHUNKS, chips - 1, piece, cols), f32),
+            pltpu.VMEM((CHUNKS, chips - 1, piece, cols), bf16),
+            pltpu.VMEM((CHUNKS, chips - 1, 2, piece, cols), bf16),
+            pltpu.VMEM((CHUNKS, chips - 1, 2, piece, cols), bf16),
+            pltpu.VMEM((2, local_ch, height, cols), bf16),
+            pltpu.SemaphoreType.DMA((CHUNKS,)),
+            pltpu.SemaphoreType.DMA((2,)),
+        ]
+        + [pltpu.SemaphoreType.DMA((c,)) for c in counts for _ in range(2)],
+        compiler_params=pltpu.CompilerParams(
+            collective_id=0, has_side_effects=True, vmem_limit_bytes=60 * 1000 * 1000
+        ),
+        name="tokens",
+    )(fields, norm_gain, fwd)
+
+
 def mix_pair(a_ref, b_ref, w_ref, b1_ref, odd, start, groups, edge):
     width = b_ref.shape[0]
     cols = b_ref.shape[3]
@@ -407,13 +562,11 @@
 def main_kernel(
     plan,
     x_ref,
-    stats_ref,
-    gain_ref,
+    along_ref,
     shift_ref,
     first_ref,
     second_ref,
     bias_ref,
-    fwd_ref,
     turn_ref,
     back_ref,
     inv_ref,
@@ -441,12 +594,9 @@
         lift_scale = float(cols * rows) * float(fwd_first(cols)) * float(fwd_first(rows))
         for n in range(0, count, 2):
             pair = [
-                normal_modes(
-                    x_ref,
-                    stats_ref,
+                turn_rows(
+                    along_ref,
                     n + i,
-                    gain_ref[index * width + here + n + i],
-                    fwd_ref,
                     turn_ref,
                     shift_ref[index * width + here + n + i] * lift_scale,
                 )
@@ -485,10 +635,11 @@
     return pl.BlockSpec(array.shape, lambda *_: zeros)
 
 
-def mix_tokens(fields, stats, norm_gain, norm_shift, first_weight, second_weight, first_bias):
+def per_device_local(fields, norm_gain, norm_shift, first_weight, second_weight, first_bias):
     local_ch, rows, cols = fields.shape
     half_r, half_c = rows // 2, cols // 2
-    tables = [jnp.asarray(t) for t in split_tables(rows, cols)]
+    fwd, *tables = (jnp.asarray(t) for t in split_tables(rows, cols))
+    along = token_rows(fields, norm_gain, fwd, lax.axis_size("grid"))
     size = first_weight.shape[2] * SUB
     per = 4 if local_ch % 4 == 0 else 2
     steps = local_ch // per
@@ -496,21 +647,17 @@
     mixes = half_r // SUB // minis
     image = jax.ShapeDtypeStruct(fields.shape, jnp.bfloat16)
     last = steps - 1
-    x_spec = pl.BlockSpec(
-        (per, rows, cols),
-        lambda i: (jnp.where(i < steps, i, jnp.maximum(i - steps - mixes, 0)), 0, 0),
-    )
-    out_spec = pl.BlockSpec(
-        (per, rows, cols), lambda i: (jnp.maximum(i - steps - mixes, 0), 0, 0)
-    )
+    block = (per, rows, cols)
+    along_spec = pl.BlockSpec(block, lambda i: (jnp.minimum(i, last), 0, 0))
+    late_spec = pl.BlockSpec(block, lambda i: (jnp.maximum(i - steps - mixes, 0), 0, 0))
     smem = pl.BlockSpec(memory_space=pltpu.SMEM)
     return pl.pallas_call(
         functools.partial(main_kernel, (steps, mixes, minis)),
         grid=(2 * steps + mixes,),
         out_shape=image,
-        in_specs=[x_spec, whole_spec(stats), smem, smem]
+        in_specs=[late_spec, along_spec, smem]
         + [whole_spec(t) for t in (first_weight, second_weight, first_bias, *tables)],
-        out_specs=out_spec,
+        out_specs=late_spec,
         scratch_shapes=[
             pltpu.VMEM((4 * half_r // SUB, size, half_c), jnp.bfloat16),
             pltpu.VMEM((local_ch, 4, half_r, half_c), jnp.bfloat16),
@@ -524,29 +671,15 @@
             flops=6 * fields.size * rows, bytes_accessed=6 * fields.size, transcendentals=0
         ),
         name="main",
-    )(fields, stats, norm_gain, norm_shift, first_weight, second_weight, first_bias, *tables)
-
-
-def per_device_local(fields, norm_gain, norm_shift, first_weight, second_weight, first_bias):
-    groups = lax.axis_size("grid")
-    values = fields.astype(jnp.float32)
-    stats = shared_stats(
-        jnp.sum(values, axis=0),
-        jnp.sum(values * values, axis=0),
-        groups,
-        fields.shape[0] * groups,
-    )
-    return mix_tokens(
-        fields, stats, norm_gain, norm_shift, first_weight, second_weight, first_bias
-    )
+    )(fields, along, norm_shift, first_weight, second_weight, first_bias, *tables)
 
 
 def per_device_any(fields, norm_gain, norm_shift, first_weight, second_weight, first_bias):
     local_ch, rows, cols = fields.shape
     groups = lax.axis_size("grid")
-    one_block = local_ch == first_weight.shape[2] and local_ch % 2 == 0
+    one_block = local_ch == first_weight.shape[2] and local_ch % TOGETHER == 0
     tiled = rows % 256 == 0 and cols % 512 == 0 and local_ch * rows * cols <= 8 * 1024 * 1024
-    tiled = tiled and groups % 2 == 0 and rows % (8 * groups) == 0
+    tiled = tiled and groups % 2 == 0 and groups >= 4 and rows % (64 * groups) == 0
     chosen = per_device_local if one_block and tiled else per_device
     return chosen(fields, norm_gain, norm_shift, first_weight, second_weight, first_bias)
 

time: 93.2 us -> 76.9 us (0.83)
  other arithmetic: 7.54 us -> 0 us
  Pallas kernels: 84 us -> 76.5 us
  local copies, waits for them, and re-layouts: 1.34 us -> 0 us
    reduce_sum x1 -> x0, other arithmetic: 7.54 us -> none  [per_device_local(): jnp.sum(values * values, axis=0)]
    pallas_call x2, Pallas kernels: 84 us -> 76.5 us  [the longest x1 41.8 us: per_device_local(): pl.pallas_call(functools.partial(main_kernel, (steps, mixes, minis)), gri...]
    unnamed x2 -> x0, local copies, waits for them, and re-layouts: 1.34 us -> none
where the time goes in v2:
time: 76.9 us; the launch traced here: 76.5 us
  Pallas kernels  76.5 us (99%)
    pallas_call x1, Pallas kernels, per_device_local(): pl.pallas_call(functools.partial(main_kernel, (steps, mixes, minis)), gri...  41.8 us
    pallas_call x1, Pallas kernels, token_rows(): pl.pallas_call(functools.partial(token_kernel, n), out_shape=jax.ShapeDty...  34.6 us

profile of v2, /device:TPU:0, one launch (start us, length us, event | category | flops | bytes accessed | tf_op | source)
XLA Modules:
  0.0 76.5 jit_solution(6337159140077919191)
XLA Ops:
  0.0 34.6 %tokens.1.along_ref = bf16[32,512,512]{2,1,0:T(8,128)(2,1)} custom-call(bf16[32,512,512]{2,1,0:T(8,128)(2,1)} %x_ref.1, f32[256]{0:T(256)} %gain_ref.1, bf16[2,256,256]{2,1,0:T(8,128)(2,1)} %constant.8.clone.fwd_ref), custom_call_target="tpu_custom_call" | custom-call | tf_op jit(solution)/shard_map/tokens/pallas_call | solution.py:477
  34.6 41.8 %main.1 = bf16[32,512,512]{2,1,0:T(8,128)(2,1)} custom-call(bf16[32,512,512]{2,1,0:T(8,128)(2,1)} %x_ref.1, bf16[32,512,512]{2,1,0:T(8,128)(2,1)} %tokens.1.along_ref, f32[256]{0:T(256)} %shift_ref.1, bf16[2,8,32,32]{3,2,1,0:T(8,128)(2,1)} %first_ref.1, bf16[2,8,32,32]{3,2,1,0:T(8,128)(2,1)} %second_ref.1, f32[2,256]{1,0:T(2,128)} %bias_ref.1, ...), custom_call_target="tpu_custom_call" | custom-call | flops 25769803776 | bytes 50331648 | tf_op jit(solution)/shard_map/main/pallas_call | solution.py:654

commit v3 on v2

--- a/solution.py
+++ b/solution.py
@@ -252,6 +252,7 @@
 
 
 CHUNKS = 4
+STARTS = (0, 1, 2, 3, 4)
 TOGETHER = 4
 
 
@@ -260,8 +261,8 @@
     x_hbm,
     gain_ref,
     fwd_ref,
-    along_hbm,
     x_ref,
+    along_ref,
     sums,
     stats,
     near,
@@ -271,9 +272,7 @@
     far_m,
     ag_out,
     ag_in,
-    stage,
     load_sem,
-    store_sem,
     s1,
     r1,
     s2,
@@ -330,7 +329,7 @@
             barrier, inc=1, device_id={"grid": device}, device_id_type=pl.DeviceIdType.MESH
         )
 
-    first, second, third, fourth, stores = {}, {}, {}, {}, {}
+    first, second, third, fourth = {}, {}, {}, {}
 
     def add_local(c):
         loads[c].wait()
@@ -421,9 +420,6 @@
 
     def transform(c):
         fourth[c].wait_recv()
-        slot = c % 2
-        if c >= 2:
-            stores[c - 2].wait()
         at = slice(c * height, (c + 1) * height)
 
         def body(i, carry):
@@ -444,24 +440,18 @@
                     fwd_ref[side],
                     preferred_element_type=jnp.float32,
                 )
-                stage[
-                    slot, pl.ds(i * TOGETHER, TOGETHER), :, side * half_c : (side + 1) * half_c
+                along_ref[
+                    pl.ds(i * TOGETHER, TOGETHER), at, side * half_c : (side + 1) * half_c
                 ] = along.reshape(TOGETHER, height, half_c).astype(jnp.bfloat16)
             return carry
 
         lax.fori_loop(0, local_ch // TOGETHER, body, 0)
-        stores[c] = pltpu.make_async_copy(
-            stage.at[slot], along_hbm.at[:, at], store_sem.at[slot]
-        )
-        stores[c].start()
 
     stages = (add_local, add_chip, finish, collect, transform)
-    for tick in range(CHUNKS + len(stages) - 1):
-        for depth, stage_of in enumerate(stages):
-            if 0 <= tick - depth < CHUNKS:
-                stage_of(tick - depth)
-    for c in range(max(CHUNKS - 2, 0), CHUNKS):
-        stores[c].wait()
+    for tick in range(CHUNKS + sum(STARTS)):
+        for stage_of, start in zip(stages, STARTS):
+            if 0 <= tick - start < CHUNKS:
+                stage_of(tick - start)
     for c in range(CHUNKS):
         for copy in [first[c], fourth[c]] + second[c] + third[c]:
             copy.wait_send()
@@ -476,15 +466,14 @@
     f32, bf16 = jnp.float32, jnp.bfloat16
     return pl.pallas_call(
         functools.partial(token_kernel, n),
-        out_shape=jax.ShapeDtypeStruct(fields.shape, bf16),
+        out_shape=[pltpu.VMEM(fields.shape, bf16)] * 2,
         in_specs=[
             pl.BlockSpec(memory_space=pl.ANY),
             pl.BlockSpec(memory_space=pltpu.SMEM),
             pl.BlockSpec(memory_space=pltpu.VMEM),
         ],
-        out_specs=pl.BlockSpec(memory_space=pl.ANY),
+        out_specs=[pl.BlockSpec(memory_space=pltpu.VMEM)] * 2,
         scratch_shapes=[
-            pltpu.VMEM(fields.shape, bf16),
             pltpu.VMEM((2, rows, cols), f32),
             pltpu.VMEM((2, rows, cols), f32),
             pltpu.VMEM((CHUNKS, 2, half, cols), f32),
@@ -494,21 +483,19 @@
             pltpu.VMEM((CHUNKS, chips - 1, piece, cols), bf16),
             pltpu.VMEM((CHUNKS, chips - 1, 2, piece, cols), bf16),
             pltpu.VMEM((CHUNKS, chips - 1, 2, piece, cols), bf16),
-            pltpu.VMEM((2, local_ch, height, cols), bf16),
             pltpu.SemaphoreType.DMA((CHUNKS,)),
-            pltpu.SemaphoreType.DMA((2,)),
         ]
         + [pltpu.SemaphoreType.DMA((c,)) for c in counts for _ in range(2)],
         compiler_params=pltpu.CompilerParams(
-            collective_id=0, has_side_effects=True, vmem_limit_bytes=60 * 1000 * 1000
+            collective_id=0, has_side_effects=True, vmem_limit_bytes=28 * 1024 * 1024
         ),
         name="tokens",
     )(fields, norm_gain, fwd)
 
 
 def mix_pair(a_ref, b_ref, w_ref, b1_ref, odd, start, groups, edge):
-    width = b_ref.shape[0]
-    cols = b_ref.shape[3]
+    width, rows, cols = b_ref.shape
+    half_r, half_c = rows // 2, cols // 2
     sums, gaps = [], []
     for g in range(2):
         mixed = []
@@ -518,7 +505,7 @@
             hid = (hid + b1_ref[...]).astype(jnp.bfloat16)
             hid = jnp.maximum(hid, jnp.zeros_like(hid))
             out = jnp.dot(w_ref[2 + side], hid, preferred_element_type=jnp.float32)
-            mixed.append((out - jnp.clip(out, -0.01, 0.01)).reshape(width, SUB, cols))
+            mixed.append((out - jnp.clip(out, -0.01, 0.01)).reshape(width, SUB, half_c))
         total, gap = mixed[0] + mixed[1], mixed[0] - mixed[1]
         if edge is not None and g == 0:
             line = lax.broadcasted_iota(jnp.int32, total.shape, 1)
@@ -528,19 +515,25 @@
             gap = jnp.where(re_edge, -moved, jnp.where(im_edge, mixed[0], gap))
         sums.append(total)
         gaps.append(gap)
-    spot = pl.ds(pl.multiple_of(start * SUB, 2 * SUB), 2 * SUB)
+    spot = pl.ds(pl.multiple_of(odd * half_r + start * SUB, 2 * SUB), 2 * SUB)
     for i, parts in enumerate((sums, gaps)):
-        b_ref[:, 2 * odd + i, spot, :] = jnp.concatenate(parts, axis=1).astype(jnp.bfloat16)
-
-
-def return_rows(x_ref, n, b_ref, channel, back_ref, inv_ref, out_ref):
-    rows, cols = x_ref.shape[1:]
-    half_c = cols // 2
+        b_ref[:, spot, i * half_c : (i + 1) * half_c] = jnp.concatenate(parts, axis=1).astype(
+            jnp.bfloat16
+        )
+
+
+def return_rows(x_ref, b_ref, channel, back_ref, inv_ref, out_ref):
+    local_ch, rows, cols = x_ref.shape
+    half_r, half_c = rows // 2, cols // 2
     quarter = half_c // 2
     parts = []
     for p in range(2):
         even, odd = (
-            jnp.dot(back_ref[2 * i + p], b_ref[channel, 2 * i + p], preferred_element_type=jnp.float32)
+            jnp.dot(
+                back_ref[2 * i + p],
+                b_ref[channel, i * half_r : (i + 1) * half_r, p * half_c : (p + 1) * half_c],
+                preferred_element_type=jnp.float32,
+            )
             for i in range(2)
         )
         parts.append(jnp.concatenate([even + odd, even - odd], axis=0).astype(jnp.bfloat16))
@@ -554,124 +547,158 @@
     )
     for i, filtered in enumerate((even + odd, even - odd)):
         span = slice(i * half_c, (i + 1) * half_c)
-        out_ref[n, :, span] = (x_ref[n, :, span].astype(jnp.float32) + filtered).astype(
-            jnp.bfloat16
-        )
+        for j in range(2):
+            line = slice(j * half_r, (j + 1) * half_r)
+            out_ref[(2 * j + i) * local_ch + channel] = (
+                x_ref[channel, line, span].astype(jnp.float32) + filtered[line]
+            ).astype(jnp.bfloat16)
 
 
 def main_kernel(
     plan,
     x_ref,
-    along_ref,
+    along_in,
     shift_ref,
     first_ref,
     second_ref,
     bias_ref,
+    turn_hbm,
+    back_hbm,
+    inv_hbm,
+    out_hbm,
+    b_ref,
+    a_ref,
     turn_ref,
     back_ref,
     inv_ref,
-    out_ref,
-    a_ref,
-    b_ref,
     w_ref,
     b1_ref,
+    store_sem,
+    table_sem,
 ):
-    steps, mixes, minis = plan
-    step = pl.program_id(0)
-    count, rows, cols = x_ref.shape
-    half_r = rows // 2
+    count, minis = plan
+    local_ch, rows, cols = x_ref.shape
+    steps = local_ch // count
+    half_r, half_c = rows // 2, cols // 2
     groups = half_r // SUB
-    width = first_ref.shape[2]
     index = lax.axis_index("grid")
-
-    @pl.when(step == 0)
-    def _():
-        prepare(index, first_ref, second_ref, bias_ref, w_ref, b1_ref)
-
-    @pl.when(step < steps)
-    def _():
-        here = step * count
-        lift_scale = float(cols * rows) * float(fwd_first(cols)) * float(fwd_first(rows))
+    tables = [
+        pltpu.make_async_copy(source, target, table_sem.at[i])
+        for i, (source, target) in enumerate(
+            ((turn_hbm, turn_ref), (back_hbm, back_ref), (inv_hbm, inv_ref))
+        )
+    ]
+
+    def result(i):
+        at = pl.ds(i * count, count)
+        return [
+            pltpu.make_async_copy(
+                a_ref.at[pl.ds((2 * j + k) * local_ch + i * count, count)],
+                out_hbm.at[
+                    at, j * half_r : (j + 1) * half_r, k * half_c : (k + 1) * half_c
+                ],
+                store_sem.at[i * 4 + 2 * j + k],
+            )
+            for j in range(2)
+            for k in range(2)
+        ]
+
+    for table in tables:
+        table.start()
+    prepare(index, first_ref, second_ref, bias_ref, w_ref, b1_ref)
+    tables[0].wait()
+    lift_scale = float(cols * rows) * float(fwd_first(cols)) * float(fwd_first(rows))
+
+    def forward(i, carry):
         for n in range(0, count, 2):
+            here = i * count + n
             pair = [
                 turn_rows(
-                    along_ref,
-                    n + i,
+                    b_ref,
+                    here + u,
                     turn_ref,
-                    shift_ref[index * width + here + n + i] * lift_scale,
+                    shift_ref[index * local_ch + here + u] * lift_scale,
                 )
-                for i in range(2)
+                for u in range(2)
             ]
-            spot = pl.ds(pl.multiple_of((here + n) * SUB, 2 * SUB), 2 * SUB)
+            spot = pl.ds(pl.multiple_of(here * SUB, 2 * SUB), 2 * SUB)
             for kind in range(4):
                 both = [p[kind].reshape(groups, SUB, -1) for p in pair]
                 a_ref[kind * groups : (kind + 1) * groups, spot, :] = jnp.concatenate(
                     both, axis=1
                 ).astype(jnp.bfloat16)
-
-    @pl.when((step >= steps) & (step < steps + mixes))
-    def _():
-        now = step - steps
+        return carry
+
+    lax.fori_loop(0, steps, forward, 0)
+
+    def mix(i, carry):
         for u in range(minis):
-            mini = now * minis + u
+            mini = i * minis + u
             odd, start = lax.div(mini, groups // 2), 2 * lax.rem(mini, groups // 2)
             mix_pair(
-                a_ref, b_ref, w_ref, b1_ref, odd, start, groups, now == 0 if u == 0 else None
+                a_ref, b_ref, w_ref, b1_ref, odd, start, groups, i == 0 if u == 0 else None
             )
-
-    @pl.when(step >= steps + mixes)
-    def _():
-        here = (step - steps - mixes) * count
+        return carry
+
+    lax.fori_loop(0, groups // minis, mix, 0)
+    for table in tables[1:]:
+        table.wait()
+
+    def backward(i, carry):
         for n in range(count):
-            return_rows(x_ref, n, b_ref, here + n, back_ref, inv_ref, out_ref)
+            return_rows(x_ref, b_ref, i * count + n, back_ref, inv_ref, a_ref)
+        for copy in result(i):
+            copy.start()
+        return carry
+
+    lax.fori_loop(0, steps, backward, 0)
+    for i in range(steps):
+        for copy in result(i):
+            copy.wait()
 
 
 def fwd_first(size):
     return np.asarray(np.float32(1.0 / math.sqrt(size))).astype(jnp.bfloat16).astype(np.float32)
-
-
-def whole_spec(array):
-    zeros = (0,) * array.ndim
-    return pl.BlockSpec(array.shape, lambda *_: zeros)
 
 
 def per_device_local(fields, norm_gain, norm_shift, first_weight, second_weight, first_bias):
     local_ch, rows, cols = fields.shape
     half_r, half_c = rows // 2, cols // 2
     fwd, *tables = (jnp.asarray(t) for t in split_tables(rows, cols))
-    along = token_rows(fields, norm_gain, fwd, lax.axis_size("grid"))
+    near = pltpu.VMEM
+    kept = [
+        pltpu.with_memory_space_constraint(t, near)
+        for t in token_rows(fields, norm_gain, fwd, lax.axis_size("grid"))
+    ]
     size = first_weight.shape[2] * SUB
-    per = 4 if local_ch % 4 == 0 else 2
-    steps = local_ch // per
-    minis = 4
-    mixes = half_r // SUB // minis
-    image = jax.ShapeDtypeStruct(fields.shape, jnp.bfloat16)
-    last = steps - 1
-    block = (per, rows, cols)
-    along_spec = pl.BlockSpec(block, lambda i: (jnp.minimum(i, last), 0, 0))
-    late_spec = pl.BlockSpec(block, lambda i: (jnp.maximum(i - steps - mixes, 0), 0, 0))
+    count, minis = 4, 4
+    steps = local_ch // count
     smem = pl.BlockSpec(memory_space=pltpu.SMEM)
-    return pl.pallas_call(
-        functools.partial(main_kernel, (steps, mixes, minis)),
-        grid=(2 * steps + mixes,),
-        out_shape=image,
-        in_specs=[late_spec, along_spec, smem]
-        + [whole_spec(t) for t in (first_weight, second_weight, first_bias, *tables)],
-        out_specs=late_spec,
+    far = pl.BlockSpec(memory_space=pl.ANY)
+    held = pl.BlockSpec(memory_space=near)
+    result, _ = pl.pallas_call(
+        functools.partial(main_kernel, (count, minis)),
+        out_shape=[jax.ShapeDtypeStruct(fields.shape, jnp.bfloat16)]
+        + [near(fields.shape, jnp.bfloat16)],
+        in_specs=[held, held, smem, held, held, held, far, far, far],
+        out_specs=[far, held],
+        input_output_aliases={1: 1},
         scratch_shapes=[
             pltpu.VMEM((4 * half_r // SUB, size, half_c), jnp.bfloat16),
-            pltpu.VMEM((local_ch, 4, half_r, half_c), jnp.bfloat16),
+        ]
+        + [pltpu.VMEM(t.shape, jnp.bfloat16) for t in tables]
+        + [
             pltpu.VMEM((4, size, size), jnp.bfloat16),
             pltpu.VMEM((size, half_c), jnp.float32),
-        ],
-        compiler_params=pltpu.CompilerParams(
-            dimension_semantics=("arbitrary",), vmem_limit_bytes=64 * 1000 * 1000
-        ),
+        ]
+        + [pltpu.SemaphoreType.DMA((c,)) for c in (4 * steps, 3)],
+        compiler_params=pltpu.CompilerParams(vmem_limit_bytes=28 * 1024 * 1024),
         cost_estimate=pl.CostEstimate(
             flops=6 * fields.size * rows, bytes_accessed=6 * fields.size, transcendentals=0
         ),
         name="main",
-    )(fields, along, norm_shift, first_weight, second_weight, first_bias, *tables)
+    )(*kept, norm_shift, first_weight, second_weight, first_bias, *tables)
+    return result
 
 
 def per_device_any(fields, norm_gain, norm_shift, first_weight, second_weight, first_bias):
@@ -679,7 +706,7 @@
     groups = lax.axis_size("grid")
     one_block = local_ch == first_weight.shape[2] and local_ch % TOGETHER == 0
     tiled = rows % 256 == 0 and cols % 512 == 0 and local_ch * rows * cols <= 8 * 1024 * 1024
-    tiled = tiled and groups % 2 == 0 and groups >= 4 and rows % (64 * groups) == 0
+    tiled = tiled and SUB * local_ch == rows // 2 and groups % 2 == 0 and groups >= 4 and rows % (64 * groups) == 0
     chosen = per_device_local if one_block and tiled else per_device
     return chosen(fields, norm_gain, norm_shift, first_weight, second_weight, first_bias)
 

time: 76.9 us -> 66.8 us (0.87)
  Pallas kernels: 76.5 us -> 66.6 us
    pallas_call x2, Pallas kernels: 76.5 us -> 66.6 us  [the longest x1 34 us: per_device_local(): pl.pallas_call(functools.partial(main_kernel, (count, minis)), out_shape=...]
where the time goes in v3:
time: 66.8 us; the launch traced here: 66.6 us
  Pallas kernels  66.6 us (100%)
    pallas_call x1, Pallas kernels, per_device_local(): pl.pallas_call(functools.partial(main_kernel, (count, minis)), out_shape=...  34 us
    pallas_call x1, Pallas kernels, token_rows(): pl.pallas_call(functools.partial(token_kernel, n), out_shape=[pltpu.VMEM(...  32.6 us

profile of v3, /device:TPU:0, one launch (start us, length us, event | category | flops | bytes accessed | tf_op | source)
XLA Modules:
  0.0 66.6 jit_solution(3947240991065753820)
XLA Ops:
  0.0 32.6 %tokens.1 = (bf16[32,512,512]{2,1,0:T(8,128)(2,1)S(1)}, bf16[32,512,512]{2,1,0:T(8,128)(2,1)S(1)}) custom-call(bf16[32,512,512]{2,1,0:T(8,128)(2,1)} %x_hbm.1, f32[256]{0:T(256)} %gain_ref.1, bf16[2,256,256]{2,1,0:T(8,128)(2,1)} %constant.8.clone.fwd_ref), custom_call_target="tpu_custom_call" | custom-call | tf_op jit(solution)/shard_map/tokens/pallas_call | solution.py:467
  32.7 34.0 %main.1 = (bf16[32,512,512]{2,1,0:T(8,128)(2,1)}, bf16[32,512,512]{2,1,0:T(8,128)(2,1)S(1)}) custom-call(bf16[32,512,512]{2,1,0:T(8,128)(2,1)S(1)} %get-tuple-element.8.x_ref, bf16[32,512,512]{2,1,0:T(8,128)(2,1)S(1)} %get-tuple-element.9.along_in, f32[256]{0:T(256)} %shift_ref.1, bf16[2,8,32,32]{3,2,1,0:T(8,128)(2,1)} %first_ref.1, ...), custom_call_target="tpu_custom_call", output_to_operand_aliasing={{1}: (1, {})} | custom-call | flops 25769803776 | bytes 50331648 | tf_op jit(solution)/shard_map/main/pallas_call | solution.py:679

commit v4 on v3

--- a/solution.py
+++ b/solution.py
@@ -235,11 +235,18 @@
     return [f.astype(jnp.bfloat16) for f in flips]
 
 
-def prepare(block, first_ref, second_ref, bias_ref, w_ref, b1_ref):
+def prepare(block, gain_ref, first_ref, second_ref, bias_ref, w_ref, b1_ref):
     width = first_ref.shape[2]
     size = width * SUB
+    row = lax.broadcasted_iota(jnp.int32, (width, width), 0)
+    gain = jnp.zeros((width, width), jnp.float32)
+    for i in range(width):
+        gain = jnp.where(row == i, gain_ref[block * width + i], gain)
     for i, (source, flip) in enumerate(((first_ref, True), (second_ref, False))):
-        pair = wide_weight(source[0, block], source[1, block], flip, not flip)
+        parts = [source[p, block] for p in range(2)]
+        if i == 0:
+            parts = [(p.astype(jnp.float32) * gain).astype(jnp.bfloat16) for p in parts]
+        pair = wide_weight(*parts, flip, not flip)
         for j in range(2):
             w_ref[2 * i + j] = pair[j]
     shape = (size, bias_ref.shape[1])
@@ -252,24 +259,21 @@
 
 
 CHUNKS = 4
-STARTS = (0, 1, 2, 3, 4)
-TOGETHER = 4
+STARTS = (0, 1, 4, 8, 9)
+TOGETHER = 16
 
 
 def token_kernel(
     n,
     x_hbm,
-    gain_ref,
     fwd_ref,
     x_ref,
     along_ref,
     sums,
     stats,
     near,
-    part_s,
-    part_m,
-    far_s,
-    far_m,
+    part,
+    far,
     ag_out,
     ag_in,
     load_sem,
@@ -301,6 +305,15 @@
     def halves(c, owner):
         return pl.ds(pl.multiple_of(c * height + owner * half, half), half)
 
+    def total_of(ref, c, j):
+        return ref[c, j, 0].astype(jnp.float32) + ref[c, j, 1].astype(jnp.float32)
+
+    def keep(at, mean, scale):
+        high = mean.astype(jnp.bfloat16)
+        stats[0, at] = high
+        stats[1, at] = (mean - high.astype(jnp.float32)).astype(jnp.bfloat16)
+        stats[2, at] = scale
+
     def send(source, target, send_sem, recv_sem, device):
         copy = pltpu.make_async_remote_copy(
             src_ref=source,
@@ -361,36 +374,41 @@
             local = pl.ds(pl.multiple_of(k * piece, piece), piece)
             total = sums[0, span(c, core, k)] + near[c, 0, local]
             square = sums[1, span(c, core, k)] + near[c, 1, local]
-            part_s[c, j - 1] = total
-            part_m[c, j - 1] = (square - total * total * (1.0 / share)).astype(jnp.bfloat16)
+            high = total.astype(jnp.bfloat16)
+            low = (total - high.astype(jnp.float32)).astype(jnp.bfloat16)
+            spread = (square - total * total * (1.0 / share)).astype(jnp.bfloat16)
+            for i, plane in enumerate((high, low, spread)):
+                part[c, j - 1, i] = plane
         second[c] = []
         for j in range(1, chips):
-            device = ahead(j) * 2 + core
-            for i, (source, target) in enumerate(((part_s, far_s), (part_m, far_m))):
-                at = (c * (chips - 1) + j - 1) * 2 + i
-                second[c].append(
-                    send(source.at[c, j - 1], target.at[c, j - 1], s2.at[at], r2.at[at], device)
+            at = c * (chips - 1) + j - 1
+            second[c].append(
+                send(
+                    part.at[c, j - 1],
+                    far.at[c, j - 1],
+                    s2.at[at],
+                    r2.at[at],
+                    ahead(j) * 2 + core,
                 )
+            )
 
     def finish(c):
         for copy in second[c]:
             copy.wait_recv()
-        own = part_s[c, chips - 1]
-        others = [far_s[c, j] for j in range(chips - 1)]
+        own = total_of(part, c, chips - 1)
+        others = [total_of(far, c, j) for j in range(chips - 1)]
         total = own
         for other in others:
             total = total + other
         mean = total * (1.0 / (share * chips))
-        spread = part_m[c, chips - 1].astype(jnp.float32)
+        spread = part[c, chips - 1, 2].astype(jnp.float32)
         for j in range(chips - 1):
-            spread = spread + far_m[c, j].astype(jnp.float32)
+            spread = spread + far[c, j, 2].astype(jnp.float32)
         gaps = [mean - other * (1.0 / share) for other in others]
         for gap in gaps + [mean - own * (1.0 / share)]:
             spread = spread + gap * gap * share
         scale = lax.rsqrt(spread * (1.0 / (share * chips)) + 1e-05)
-        mine = span(c, core, chip)
-        stats[0, mine] = mean
-        stats[1, mine] = scale
+        keep(span(c, core, chip), mean, scale.astype(jnp.bfloat16))
         third[c] = []
         for j in range(1, chips):
             ag_out[c, j - 1, 0] = gaps[j - 1].astype(jnp.bfloat16)
@@ -411,10 +429,9 @@
         for copy in third[c]:
             copy.wait_recv()
         for j in range(1, chips):
-            at = span(c, core, ahead(j))
             gap = ag_in[c, j - 1, 0].astype(jnp.float32)
-            stats[0, at] = part_s[c, j - 1] * (1.0 / share) + gap
-            stats[1, at] = ag_in[c, j - 1, 1].astype(jnp.float32)
+            mean = total_of(part, c, j - 1) * (1.0 / share) + gap
+            keep(span(c, core, ahead(j)), mean, ag_in[c, j - 1, 1])
         block = stats.at[:, halves(c, core)]
         fourth[c] = send(block, block, s4.at[c], r4.at[c], sibling)
 
@@ -426,11 +443,8 @@
             sides = [[], []]
             for u in range(TOGETHER):
                 ch = i * TOGETHER + u
-                value = x_ref[ch, at, :].astype(jnp.float32)
-                gain = gain_ref[me * local_ch + ch]
-                normed = ((value - stats[0, at, :]) * stats[1, at, :] * gain).astype(
-                    jnp.bfloat16
-                )
+                value = (x_ref[ch, at, :] - stats[0, at, :]) - stats[1, at, :]
+                normed = value * stats[2, at, :]
                 left, right = normed[:, :half_c], normed[:, half_c:]
                 sides[0].append(left + right)
                 sides[1].append(left - right)
@@ -457,30 +471,27 @@
             copy.wait_send()
 
 
-def token_rows(fields, norm_gain, fwd, n):
+def token_rows(fields, fwd, n):
     local_ch, rows, cols = fields.shape
     chips = n // 2
     height = rows // CHUNKS
     half, piece = height // 2, height // n
-    counts = (CHUNKS, CHUNKS * (chips - 1) * 2, CHUNKS * (chips - 1), CHUNKS)
+    counts = (CHUNKS, CHUNKS * (chips - 1), CHUNKS * (chips - 1), CHUNKS)
     f32, bf16 = jnp.float32, jnp.bfloat16
     return pl.pallas_call(
         functools.partial(token_kernel, n),
         out_shape=[pltpu.VMEM(fields.shape, bf16)] * 2,
         in_specs=[
             pl.BlockSpec(memory_space=pl.ANY),
-            pl.BlockSpec(memory_space=pltpu.SMEM),
             pl.BlockSpec(memory_space=pltpu.VMEM),
         ],
         out_specs=[pl.BlockSpec(memory_space=pltpu.VMEM)] * 2,
         scratch_shapes=[
             pltpu.VMEM((2, rows, cols), f32),
-            pltpu.VMEM((2, rows, cols), f32),
+            pltpu.VMEM((3, rows, cols), bf16),
             pltpu.VMEM((CHUNKS, 2, half, cols), f32),
-            pltpu.VMEM((CHUNKS, chips, piece, cols), f32),
-            pltpu.VMEM((CHUNKS, chips, piece, cols), bf16),
-            pltpu.VMEM((CHUNKS, chips - 1, piece, cols), f32),
-            pltpu.VMEM((CHUNKS, chips - 1, piece, cols), bf16),
+            pltpu.VMEM((CHUNKS, chips, 3, piece, cols), bf16),
+            pltpu.VMEM((CHUNKS, chips - 1, 3, piece, cols), bf16),
             pltpu.VMEM((CHUNKS, chips - 1, 2, piece, cols), bf16),
             pltpu.VMEM((CHUNKS, chips - 1, 2, piece, cols), bf16),
             pltpu.SemaphoreType.DMA((CHUNKS,)),
@@ -490,7 +501,7 @@
             collective_id=0, has_side_effects=True, vmem_limit_bytes=28 * 1024 * 1024
         ),
         name="tokens",
-    )(fields, norm_gain, fwd)
+    )(fields, fwd)
 
 
 def mix_pair(a_ref, b_ref, w_ref, b1_ref, odd, start, groups, edge):
@@ -558,6 +569,7 @@
     plan,
     x_ref,
     along_in,
+    gain_ref,
     shift_ref,
     first_ref,
     second_ref,
@@ -605,20 +617,18 @@
 
     for table in tables:
         table.start()
-    prepare(index, first_ref, second_ref, bias_ref, w_ref, b1_ref)
+    prepare(index, gain_ref, first_ref, second_ref, bias_ref, w_ref, b1_ref)
     tables[0].wait()
     lift_scale = float(cols * rows) * float(fwd_first(cols)) * float(fwd_first(rows))
+
+    def lift(channel):
+        return shift_ref[channel] / gain_ref[channel] * lift_scale
 
     def forward(i, carry):
         for n in range(0, count, 2):
             here = i * count + n
             pair = [
-                turn_rows(
-                    b_ref,
-                    here + u,
-                    turn_ref,
-                    shift_ref[index * local_ch + here + u] * lift_scale,
-                )
+                turn_rows(b_ref, here + u, turn_ref, lift(index * local_ch + here + u))
                 for u in range(2)
             ]
             spot = pl.ds(pl.multiple_of(here * SUB, 2 * SUB), 2 * SUB)
@@ -668,10 +678,10 @@
     near = pltpu.VMEM
     kept = [
         pltpu.with_memory_space_constraint(t, near)
-        for t in token_rows(fields, norm_gain, fwd, lax.axis_size("grid"))
+        for t in token_rows(fields, fwd, lax.axis_size("grid"))
     ]
     size = first_weight.shape[2] * SUB
-    count, minis = 4, 4
+    count, minis = 4, 16
     steps = local_ch // count
     smem = pl.BlockSpec(memory_space=pltpu.SMEM)
     far = pl.BlockSpec(memory_space=pl.ANY)
@@ -680,7 +690,7 @@
         functools.partial(main_kernel, (count, minis)),
         out_shape=[jax.ShapeDtypeStruct(fields.shape, jnp.bfloat16)]
         + [near(fields.shape, jnp.bfloat16)],
-        in_specs=[held, held, smem, held, held, held, far, far, far],
+        in_specs=[held, held, smem, smem, held, held, held, far, far, far],
         out_specs=[far, held],
         input_output_aliases={1: 1},
         scratch_shapes=[
@@ -697,7 +707,7 @@
             flops=6 * fields.size * rows, bytes_accessed=6 * fields.size, transcendentals=0
         ),
         name="main",
-    )(*kept, norm_shift, first_weight, second_weight, first_bias, *tables)
+    )(*kept, norm_gain, norm_shift, first_weight, second_weight, first_bias, *tables)
     return result
 
 

time: 66.8 us -> 60.5 us (0.906)
  Pallas kernels: 66.6 us -> 60.4 us
    pallas_call x1, Pallas kernels: 32.6 us -> 28.4 us  [token_rows(): pl.pallas_call(functools.partial(token_kernel, n), out_shape=[pltpu.VMEM(...]
    pallas_call x1, Pallas kernels: 34 us -> 32 us  [per_device_local(): pl.pallas_call(functools.partial(main_kernel, (count, minis)), out_shape=...]
where the time goes in v4:
time: 60.5 us; the launch traced here: 60.4 us
  Pallas kernels  60.4 us (100%)
    pallas_call x1, Pallas kernels, per_device_local(): pl.pallas_call(functools.partial(main_kernel, (count, minis)), out_shape=...  32 us
    pallas_call x1, Pallas kernels, token_rows(): pl.pallas_call(functools.partial(token_kernel, n), out_shape=[pltpu.VMEM(...  28.4 us

profile of v4, /device:TPU:0, one launch (start us, length us, event | category | flops | bytes accessed | tf_op | source)
XLA Modules:
  0.0 60.4 jit_solution(15607086362217831624)
XLA Ops:
  0.0 28.4 %tokens.1 = (bf16[32,512,512]{2,1,0:T(8,128)(2,1)S(1)}, bf16[32,512,512]{2,1,0:T(8,128)(2,1)S(1)}) custom-call(bf16[32,512,512]{2,1,0:T(8,128)(2,1)} %x_hbm.1, bf16[2,256,256]{2,1,0:T(8,128)(2,1)} %constant.8.clone.fwd_ref), custom_call_target="tpu_custom_call" | custom-call | tf_op jit(solution)/shard_map/tokens/pallas_call | solution.py:481
  28.4 32.0 %main.1 = (bf16[32,512,512]{2,1,0:T(8,128)(2,1)}, bf16[32,512,512]{2,1,0:T(8,128)(2,1)S(1)}) custom-call(bf16[32,512,512]{2,1,0:T(8,128)(2,1)S(1)} %get-tuple-element.8.x_ref, bf16[32,512,512]{2,1,0:T(8,128)(2,1)S(1)} %get-tuple-element.9.along_in, f32[256]{0:T(256)} %gain_ref.1, f32[256]{0:T(256)} %shift_ref.1, ...), custom_call_target="tpu_custom_call", output_to_operand_aliasing={{1}: (1, {})} | custom-call | flops 25769803776 | bytes 50331648 | tf_op jit(solution)/shard_map/main/pallas_call | solution.py:689

commit v5 on v4

--- a/solution.py
+++ b/solution.py
@@ -258,9 +258,9 @@
     b1_ref[...] = jnp.broadcast_to(column, b1_ref.shape)
 
 
-CHUNKS = 4
-STARTS = (0, 1, 4, 8, 9)
-TOGETHER = 16
+CHUNKS = 8
+STARTS = (0, 1, 4, 7, 9)
+TOGETHER = 32
 
 
 def token_kernel(
@@ -293,26 +293,26 @@
     local_ch, rows, cols = x_ref.shape
     half_c = cols // 2
     height = rows // CHUNKS
-    half, piece = height // 2, height // n
+    half, piece = height // 2, cols // chips
     share = 2.0 * local_ch
 
     def ahead(j):
         return lax.rem(chip + j, chips)
 
-    def span(c, owner, k):
-        return pl.ds(pl.multiple_of(c * height + owner * half + k * piece, piece), piece)
-
     def halves(c, owner):
         return pl.ds(pl.multiple_of(c * height + owner * half, half), half)
 
+    def lanes(k):
+        return pl.ds(pl.multiple_of(k * piece, piece), piece)
+
     def total_of(ref, c, j):
         return ref[c, j, 0].astype(jnp.float32) + ref[c, j, 1].astype(jnp.float32)
 
-    def keep(at, mean, scale):
+    def keep(c, k, mean, scale):
         high = mean.astype(jnp.bfloat16)
-        stats[0, at] = high
-        stats[1, at] = (mean - high.astype(jnp.float32)).astype(jnp.bfloat16)
-        stats[2, at] = scale
+        low = (mean - high.astype(jnp.float32)).astype(jnp.bfloat16)
+        for i, plane in enumerate((high, low, scale)):
+            stats[i, halves(c, core), lanes(k)] = plane
 
     def send(source, target, send_sem, recv_sem, device):
         copy = pltpu.make_async_remote_copy(
@@ -370,10 +370,9 @@
     def add_chip(c):
         first[c].wait_recv()
         for j in range(1, chips + 1):
-            k = ahead(j)
-            local = pl.ds(pl.multiple_of(k * piece, piece), piece)
-            total = sums[0, span(c, core, k)] + near[c, 0, local]
-            square = sums[1, span(c, core, k)] + near[c, 1, local]
+            at = lanes(ahead(j))
+            total = sums[0, halves(c, core), at] + near[c, 0, :, at]
+            square = sums[1, halves(c, core), at] + near[c, 1, :, at]
             high = total.astype(jnp.bfloat16)
             low = (total - high.astype(jnp.float32)).astype(jnp.bfloat16)
             spread = (square - total * total * (1.0 / share)).astype(jnp.bfloat16)
@@ -408,7 +407,7 @@
         for gap in gaps + [mean - own * (1.0 / share)]:
             spread = spread + gap * gap * share
         scale = lax.rsqrt(spread * (1.0 / (share * chips)) + 1e-05)
-        keep(span(c, core, chip), mean, scale.astype(jnp.bfloat16))
+        keep(c, chip, mean, scale.astype(jnp.bfloat16))
         third[c] = []
         for j in range(1, chips):
             ag_out[c, j - 1, 0] = gaps[j - 1].astype(jnp.bfloat16)
@@ -431,7 +430,7 @@
         for j in range(1, chips):
             gap = ag_in[c, j - 1, 0].astype(jnp.float32)
             mean = total_of(part, c, j - 1) * (1.0 / share) + gap
-            keep(span(c, core, ahead(j)), mean, ag_in[c, j - 1, 1])
+            keep(c, ahead(j), mean, ag_in[c, j - 1, 1])
         block = stats.at[:, halves(c, core)]
         fourth[c] = send(block, block, s4.at[c], r4.at[c], sibling)
 
@@ -462,7 +461,7 @@
         lax.fori_loop(0, local_ch // TOGETHER, body, 0)
 
     stages = (add_local, add_chip, finish, collect, transform)
-    for tick in range(CHUNKS + sum(STARTS)):
+    for tick in range(CHUNKS + STARTS[-1]):
         for stage_of, start in zip(stages, STARTS):
             if 0 <= tick - start < CHUNKS:
                 stage_of(tick - start)
@@ -475,7 +474,7 @@
     local_ch, rows, cols = fields.shape
     chips = n // 2
     height = rows // CHUNKS
-    half, piece = height // 2, height // n
+    half, piece = height // 2, cols // chips
     counts = (CHUNKS, CHUNKS * (chips - 1), CHUNKS * (chips - 1), CHUNKS)
     f32, bf16 = jnp.float32, jnp.bfloat16
     return pl.pallas_call(
@@ -490,10 +489,10 @@
             pltpu.VMEM((2, rows, cols), f32),
             pltpu.VMEM((3, rows, cols), bf16),
             pltpu.VMEM((CHUNKS, 2, half, cols), f32),
-            pltpu.VMEM((CHUNKS, chips, 3, piece, cols), bf16),
-            pltpu.VMEM((CHUNKS, chips - 1, 3, piece, cols), bf16),
-            pltpu.VMEM((CHUNKS, chips - 1, 2, piece, cols), bf16),
-            pltpu.VMEM((CHUNKS, chips - 1, 2, piece, cols), bf16),
+            pltpu.VMEM((CHUNKS, chips, 3, half, piece), bf16),
+            pltpu.VMEM((CHUNKS, chips - 1, 3, half, piece), bf16),
+            pltpu.VMEM((CHUNKS, chips - 1, 2, half, piece), bf16),
+            pltpu.VMEM((CHUNKS, chips - 1, 2, half, piece), bf16),
             pltpu.SemaphoreType.DMA((CHUNKS,)),
         ]
         + [pltpu.SemaphoreType.DMA((c,)) for c in counts for _ in range(2)],
@@ -588,7 +587,7 @@
     store_sem,
     table_sem,
 ):
-    count, minis = plan
+    count, minis, deep, sent = plan
     local_ch, rows, cols = x_ref.shape
     steps = local_ch // count
     half_r, half_c = rows // 2, cols // 2
@@ -602,10 +601,10 @@
     ]
 
     def result(i):
-        at = pl.ds(i * count, count)
+        at = pl.ds(i * sent, sent)
         return [
             pltpu.make_async_copy(
-                a_ref.at[pl.ds((2 * j + k) * local_ch + i * count, count)],
+                a_ref.at[pl.ds((2 * j + k) * local_ch + i * sent, sent)],
                 out_hbm.at[
                     at, j * half_r : (j + 1) * half_r, k * half_c : (k + 1) * half_c
                 ],
@@ -655,14 +654,15 @@
         table.wait()
 
     def backward(i, carry):
-        for n in range(count):
-            return_rows(x_ref, b_ref, i * count + n, back_ref, inv_ref, a_ref)
-        for copy in result(i):
-            copy.start()
+        for n in range(0, deep, sent):
+            for u in range(sent):
+                return_rows(x_ref, b_ref, i * deep + n + u, back_ref, inv_ref, a_ref)
+            for copy in result(i * (deep // sent) + n // sent):
+                copy.start()
         return carry
 
-    lax.fori_loop(0, steps, backward, 0)
-    for i in range(steps):
+    lax.fori_loop(0, local_ch // deep, backward, 0)
+    for i in range(local_ch // sent):
         for copy in result(i):
             copy.wait()
 
@@ -681,13 +681,13 @@
         for t in token_rows(fields, fwd, lax.axis_size("grid"))
     ]
     size = first_weight.shape[2] * SUB
-    count, minis = 4, 16
-    steps = local_ch // count
+    plan = (16, 16, 16, 4)
+    parts = 4 * local_ch // plan[3]
     smem = pl.BlockSpec(memory_space=pltpu.SMEM)
     far = pl.BlockSpec(memory_space=pl.ANY)
     held = pl.BlockSpec(memory_space=near)
     result, _ = pl.pallas_call(
-        functools.partial(main_kernel, (count, minis)),
+        functools.partial(main_kernel, plan),
         out_shape=[jax.ShapeDtypeStruct(fields.shape, jnp.bfloat16)]
         + [near(fields.shape, jnp.bfloat16)],
         in_specs=[held, held, smem, smem, held, held, held, far, far, far],
@@ -701,7 +701,7 @@
             pltpu.VMEM((4, size, size), jnp.bfloat16),
             pltpu.VMEM((size, half_c), jnp.float32),
         ]
-        + [pltpu.SemaphoreType.DMA((c,)) for c in (4 * steps, 3)],
+        + [pltpu.SemaphoreType.DMA((c,)) for c in (parts, 3)],
         compiler_params=pltpu.CompilerParams(vmem_limit_bytes=28 * 1024 * 1024),
         cost_estimate=pl.CostEstimate(
             flops=6 * fields.size * rows, bytes_accessed=6 * fields.size, transcendentals=0
@@ -716,7 +716,7 @@
     groups = lax.axis_size("grid")
     one_block = local_ch == first_weight.shape[2] and local_ch % TOGETHER == 0
     tiled = rows % 256 == 0 and cols % 512 == 0 and local_ch * rows * cols <= 8 * 1024 * 1024
-    tiled = tiled and SUB * local_ch == rows // 2 and groups % 2 == 0 and groups >= 4 and rows % (64 * groups) == 0
+    tiled = tiled and SUB * local_ch == rows // 2 and groups % 2 == 0 and groups >= 4 and cols % (LANE * groups // 2) == 0 and rows % (32 * CHUNKS) == 0
     chosen = per_device_local if one_block and tiled else per_device
     return chosen(fields, norm_gain, norm_shift, first_weight, second_weight, first_bias)
 

time: 60.5 us -> 58.2 us (0.962)
  Pallas kernels: 60.4 us -> 57.9 us
    pallas_call x1, Pallas kernels: 28.4 us -> 26.8 us  [token_rows(): pl.pallas_call(functools.partial(token_kernel, n), out_shape=[pltpu.VMEM(...]
    pallas_call x1, Pallas kernels: 32 us -> 31.1 us  [per_device_local(): pl.pallas_call(functools.partial(main_kernel, plan), out_shape=[jax.Shape...]
where the time goes in v5:
time: 58.2 us; the launch traced here: 58.1 us
  Pallas kernels  57.9 us (99%)
    pallas_call x1, Pallas kernels, per_device_local(): pl.pallas_call(functools.partial(main_kernel, plan), out_shape=[jax.Shape...  31.1 us
    pallas_call x1, Pallas kernels, token_rows(): pl.pallas_call(functools.partial(token_kernel, n), out_shape=[pltpu.VMEM(...  26.8 us

profile of v5, /device:TPU:0, one launch (start us, length us, event | category | flops | bytes accessed | tf_op | source)
XLA Modules:
  0.0 58.1 jit_solution(5096255608988086966)
XLA Ops:
  0.0 26.8 %tokens.1 = (bf16[32,512,512]{2,1,0:T(8,128)(2,1)S(1)}, bf16[32,512,512]{2,1,0:T(8,128)(2,1)S(1)}) custom-call(bf16[32,512,512]{2,1,0:T(8,128)(2,1)} %x_hbm.1, bf16[2,256,256]{2,1,0:T(8,128)(2,1)} %constant.8.clone.fwd_ref), custom_call_target="tpu_custom_call" | custom-call | tf_op jit(solution)/shard_map/tokens/pallas_call | solution.py:480
  26.8 31.1 %main.1 = (bf16[32,512,512]{2,1,0:T(8,128)(2,1)}, bf16[32,512,512]{2,1,0:T(8,128)(2,1)S(1)}) custom-call(bf16[32,512,512]{2,1,0:T(8,128)(2,1)S(1)} %get-tuple-element.8.x_ref, bf16[32,512,512]{2,1,0:T(8,128)(2,1)S(1)} %get-tuple-element.9.along_in, f32[256]{0:T(256)} %gain_ref.1, f32[256]{0:T(256)} %shift_ref.1, ...), custom_call_target="tpu_custom_call", output_to_operand_aliasing={{1}: (1, {})} | custom-call | flops 25769803776 | bytes 50331648 | tf_op jit(solution)/shard_map/main/pallas_call | solution.py:689
